TPU v7x, 32 devices: a whole 2x2x4 slice. The times are simulated.
32 devices in a mesh: batch: 4 (over x, core), rows: 8 (over z, y).
Axes of the slice: x: 2, y: 2, z: 4, core: 2. Of those that a mesh axis runs over, the one named last changes fastest.
Arguments:
- feat_quarter: bfloat16 [4, 128, 512, 256], P('batch', 'rows'), may hold values from -12 to 12
- feat_eighth: bfloat16 [4, 64, 256, 256], P('batch', 'rows'), may hold values from -12 to 12
- feat_sixteenth: bfloat16 [4, 32, 128, 256], P('batch', 'rows'), may hold values from -12 to 12
- feat_thirty: bfloat16 [4, 16, 64, 256], P('batch', 'rows'), may hold values from -12 to 12
- labels: int32 [4, 128, 512], P('batch', 'rows'), may hold values from 0 to 255, as said below
- first_weights: bfloat16 [4, 3, 3, 256, 128], replicated, may hold values from -0.125 to 0.125
- inner_weights: bfloat16 [3, 3, 3, 128, 128], replicated, may hold values from -0.1875 to 0.1875
- norm_gain: float32 [7, 128], replicated, may hold values from 0.1 to 1.9
- norm_shift: float32 [7, 128], replicated, may hold values from -3 to 3
- class_weight: bfloat16 [128, 19], replicated, may hold values from -0.5 to 0.5
- class_bias: float32 [19], replicated, may hold values from -3 to 3
Outputs:
- logits: bfloat16 [4, 19, 128, 512], P('batch', None, 'rows')
- mean_loss: float32 [], replicated
Inputs may be any that keep to these rules, and one draw needn't show every extreme that they name: `labels`: values 0 to 18 name classes; 255 marks a pixel without a label.
All inputs are finite; a program needn't handle non-finite values.
Results may differ from a plain program's by a relative error of at most 0.008.
Values may be sent and summed in bfloat16 or wider, within the bound.
A program may use at most 128 MiB of HBM per device.

v0:
```python
import functools

import jax
import jax.numpy as jnp
import numpy as np
from jax import lax
from jax.experimental import pallas as pl
from jax.experimental.pallas import tpu as pltpu
from jax.sharding import PartitionSpec as P

GROUPS = 32
NORM_FLOOR = 0.05
MESH = pl.DeviceIdType.MESH


def exchange_kernel(shape, axes, x_ref, out_ref, send_sem, recv_sem):
    coords = [lax.axis_index(axis) for axis in shape]
    names = list(shape)
    total = 1
    for axis in axes:
        total *= shape[axis]

    def peer(distance):
        ids = list(coords)
        rest = distance
        for axis in reversed(axes):
            size = shape[axis]
            ids[names.index(axis)] = lax.rem(coords[names.index(axis)] + rest % size, size)
            rest //= size
        return tuple(ids)

    barrier = pltpu.get_barrier_semaphore()
    for d in range(1, total):
        pl.semaphore_signal(barrier, inc=1, device_id=peer(d), device_id_type=MESH)
    pl.semaphore_wait(barrier, total - 1)
    copies = []
    for d in range(1, total):
        copy = pltpu.make_async_remote_copy(
            src_ref=x_ref,
            dst_ref=out_ref.at[d],
            send_sem=send_sem.at[d],
            recv_sem=recv_sem.at[d],
            device_id=peer(d),
            device_id_type=MESH,
        )
        copy.start()
        copies.append(copy)
    out_ref[0] = x_ref[...]
    for copy in copies:
        copy.wait()


def exchange(x, shape, axes, collective_id):
    total = 1
    for axis in axes:
        total *= shape[axis]
    return pl.pallas_call(
        functools.partial(exchange_kernel, shape, axes),
        out_shape=jax.ShapeDtypeStruct((total,) + x.shape, x.dtype),
        in_specs=[pl.BlockSpec(memory_space=pltpu.VMEM)],
        out_specs=pl.BlockSpec(memory_space=pltpu.VMEM),
        scratch_shapes=[pltpu.SemaphoreType.DMA((total,)), pltpu.SemaphoreType.DMA((total,))],
        compiler_params=pltpu.CompilerParams(collective_id=collective_id, has_side_effects=True),
    )(x)


def conv_kernel(rows, x_ref, w_ref, y_ref, stat_ref, flat_ref):
    cols, depth = x_ref.shape[1:]
    width = w_ref.shape[3]
    step = pl.program_id(0)

    @pl.when(step == 0)
    def _():
        for down in range(3):
            for across in range(3):
                flat_ref[
                    down * depth : (down + 1) * depth, across * width : (across + 1) * width
                ] = w_ref[down, across]

    lhs = jnp.concatenate(
        [
            x_ref[pl.ds(step * rows + down, rows)].reshape(rows * cols, depth)
            for down in range(3)
        ],
        axis=1,
    )
    taps = jnp.dot(lhs, flat_ref[...], preferred_element_type=jnp.float32)
    col = lax.rem(lax.broadcasted_iota(jnp.int32, (rows * cols, width), 0), cols)
    left = jnp.where(col == 0, 0.0, pltpu.roll(taps[:, :width], 1, 0))
    right = jnp.where(col == cols - 1, 0.0, pltpu.roll(taps[:, 2 * width :], rows * cols - 1, 0))
    y = (taps[:, width : 2 * width] + left + right).reshape(rows, cols, width)
    y_ref[...] = y
    sums = jnp.sum(y, axis=1, keepdims=True)
    centred = y - sums / cols
    stat_ref[:, 0:1] = sums
    stat_ref[:, 1:2] = jnp.sum(centred * centred, axis=1, keepdims=True)


def conv(framed, weight):
    count, cols, depth = framed.shape
    count -= 2
    width = weight.shape[3]
    rows = max(r for r in range(1, count + 1) if count % r == 0 and (r == 1 or r * cols <= 1024))
    return pl.pallas_call(
        functools.partial(conv_kernel, rows),
        grid=(count // rows,),
        out_shape=(
            jax.ShapeDtypeStruct((count, cols, width), jnp.float32),
            jax.ShapeDtypeStruct((count, 2, width), jnp.float32),
        ),
        in_specs=[
            pl.BlockSpec(framed.shape, lambda i: (0, 0, 0)),
            pl.BlockSpec(weight.shape, lambda i: (0, 0, 0, 0)),
        ],
        out_specs=(
            pl.BlockSpec((rows, cols, width), lambda i: (i, 0, 0)),
            pl.BlockSpec((rows, 2, width), lambda i: (i, 0, 0)),
        ),
        scratch_shapes=[pltpu.VMEM((3 * depth, 3 * width), jnp.bfloat16)],
        cost_estimate=pl.CostEstimate(
            flops=18 * count * cols * depth * width,
            bytes_accessed=2 * framed.size + 4 * count * cols * width,
            transcendentals=0,
        ),
    )(framed, weight)


def edges_kernel(size, widths, *refs):
    many = len(widths)
    arrays, before, after = refs[:many], refs[many : 2 * many], refs[2 * many : 3 * many]
    send_sem, recv_sem = refs[3 * many :]
    me = lax.axis_index("rows")
    reach = max(-(-w // a.shape[0]) for a, w in zip(arrays, widths))
    barrier = pltpu.get_barrier_semaphore()
    sides = [side * step for step in range(1, reach + 1) for side in (1, -1)]

    def exists(offset):
        return me + offset < size if offset > 0 else me + offset >= 0

    def target(offset):
        return {"rows": lax.rem(me + offset + size, size)}

    for offset in sides:

        @pl.when(exists(offset))
        def _():
            pl.semaphore_signal(
                barrier, inc=1, device_id=target(offset), device_id_type=MESH
            )

    peers = jnp.minimum(me, reach) + jnp.minimum(size - 1 - me, reach)
    pl.semaphore_wait(barrier, peers)

    copies = []
    for index in reversed(range(many)):
        array, width = arrays[index], widths[index]
        length = array.shape[0]
        done, step = 0, 1
        while done < width:
            take = min(width - done, length)
            for offset in (step, -step):
                if offset > 0:
                    source = array.at[length - take : length]
                    landing = before[index].at[width - done - take : width - done]
                else:
                    source = array.at[0:take]
                    landing = after[index].at[done : done + take]
                copy = pltpu.make_async_remote_copy(
                    src_ref=source,
                    dst_ref=landing,
                    send_sem=send_sem.at[len(copies)],
                    recv_sem=recv_sem.at[len(copies)],
                    device_id=target(offset),
                    device_id_type=MESH,
                )
                copies.append((copy, offset, landing))
                pl.when(exists(offset))(copy.start)
            done += take
            step += 1
    for copy, offset, landing in copies:

        @pl.when(jnp.logical_not(exists(-offset)))
        def _():
            landing[...] = jnp.zeros(landing.shape, landing.dtype)

        pl.when(exists(offset))(copy.wait_send)
        pl.when(exists(-offset))(copy.wait_recv)


def edges(arrays, widths, size, collective_id):
    outs = [jax.ShapeDtypeStruct((w,) + a.shape[1:], a.dtype) for a, w in zip(arrays, widths)]
    copies = 2 * sum(-(-w // a.shape[0]) for a, w in zip(arrays, widths))
    got = pl.pallas_call(
        functools.partial(edges_kernel, size, tuple(widths)),
        out_shape=tuple(outs + outs),
        in_specs=[pl.BlockSpec(memory_space=pl.ANY)] * len(arrays),
        out_specs=tuple([pl.BlockSpec(memory_space=pltpu.VMEM)] * (2 * len(arrays))),
        scratch_shapes=[pltpu.SemaphoreType.DMA((copies,)), pltpu.SemaphoreType.DMA((copies,))],
        compiler_params=pltpu.CompilerParams(collective_id=collective_id, has_side_effects=True),
    )(*arrays)
    return got[: len(arrays)], got[len(arrays) :]


def fold(values):
    return values.reshape(GROUPS, -1).sum(axis=1)


def spread(values, width):
    return jnp.repeat(values, width // GROUPS)


def double_rows(field, axis):
    count = field.shape[axis]
    first = lax.slice_in_dim(field, 0, count - 1, axis=axis)
    second = lax.slice_in_dim(field, 1, count, axis=axis)
    lines = jnp.stack([0.75 * first + 0.25 * second, 0.25 * first + 0.75 * second], axis=axis + 1)
    return lines.reshape(field.shape[:axis] + (2 * count - 2,) + field.shape[axis + 1 :])


def col_matrix(cols):
    target = np.arange(2 * cols)
    near = target // 2
    far = np.clip(near + 2 * (target % 2) - 1, 0, cols - 1)
    source = np.arange(cols)[:, None]
    return (0.75 * (source == near) + 0.25 * (source == far)).astype(np.float32)


def make_per_device(shape):
    def per_device(
        feat_quarter,
        feat_eighth,
        feat_sixteenth,
        feat_thirty,
        labels,
        first_weights,
        inner_weights,
        norm_gain,
        norm_shift,
        class_weight,
        class_bias,
    ):
        position = lax.axis_index("rows")
        size = shape["rows"]

        def statistics(fields):
            slab, counts = [], []
            for rows, cols in fields:
                width = rows.shape[2]
                count = rows.shape[0] * cols * (width // GROUPS)
                sums = rows[:, 0].sum(axis=0)
                mean = spread(fold(sums) / count, width)
                strays = cols * ((rows[:, 0] / cols - mean) ** 2).sum(axis=0)
                slab += [sums, rows[:, 1].sum(axis=0) + strays]
                counts.append(count)
            slab += [jnp.zeros_like(slab[0])] * (-len(slab) % 8)
            all_slabs = exchange(jnp.stack(slab), shape, ("rows",), 0)
            folded = all_slabs.reshape(size, -1, GROUPS, width // GROUPS).sum(axis=3)
            result = []
            for i, count in enumerate(counts):
                means = folded[:, 2 * i] / count
                mean = means.mean(axis=0)
                spread_squares = count * ((means - mean) ** 2).sum(axis=0)
                var = (folded[:, 2 * i + 1].sum(axis=0) + spread_squares) / (count * size)
                result.append((mean, var))
            return result

        def activate(y, stat, layer):
            width = y.shape[2]
            factor = norm_gain[layer] * lax.rsqrt(spread(stat[1], width) + NORM_FLOOR)
            return jnp.maximum(
                (y - spread(stat[0], width)) * factor + norm_shift[layer], 0.0
            ).astype(jnp.bfloat16)

        def rows_of(dims, own, extra):
            return position * own + lax.broadcasted_iota(jnp.int32, dims, 0) - extra

        def double(act, own, extra, kept):
            numbers = rows_of(act.shape, own, extra)
            top, bottom = act[extra : extra + 1], act[extra + own - 1 : extra + own]
            act = jnp.where(numbers < 0, top, jnp.where(numbers >= own * size, bottom, act))
            wide = jnp.einsum(
                "rwc,wv->rvc",
                act,
                jnp.asarray(col_matrix(act.shape[1]), jnp.bfloat16),
                preferred_element_type=jnp.float32,
            )
            cut = 2 * extra - 1 - kept
            grown = double_rows(wide, 0)[cut : cut + 2 * own + 2 * kept].astype(jnp.bfloat16)
            lines = rows_of(grown.shape, 2 * own, kept)
            inside = (lines >= 0) & (lines < 2 * own * size)
            return jnp.where(inside, grown, jnp.zeros_like(grown))

        q, e, s, t = feat_quarter[0], feat_eighth[0], feat_sixteenth[0], feat_thirty[0]
        t_own, s_own, e_own = t.shape[0], s.shape[0], e.shape[0]
        bands = [q, e, s, t]
        q_framed, e_framed, s_framed, t_framed = [
            jnp.concatenate([x, band, z], axis=0)
            for x, band, z in zip(*((lambda g: (g[0], bands, g[1]))(edges(bands, [1, 1, 2, 3], size, 2))))
        ]
        t_out, t_sum = conv(t_framed, first_weights[3])
        s_out, s_sum = conv(s_framed, first_weights[2])
        t_stat, s_stat = statistics([(t_sum[2:-2], t_out.shape[1]), (s_sum[1:-1], s_out.shape[1])])
        t_out, t_sum = conv(double(activate(t_out, t_stat, 3), t_own, 2, 2), inner_weights[1])
        s_out, s_sum = conv(double(activate(s_out, s_stat, 2), s_own, 1, 1), inner_weights[0])
        e_out, e_sum = conv(e_framed, first_weights[1])
        t_stat, s_stat, e_stat = statistics(
            [(t_sum[1:-1], t_out.shape[1]), (s_sum, s_out.shape[1]), (e_sum, e_out.shape[1])]
        )
        s_act = activate(s_out, s_stat, 4)
        e_act = activate(e_out, e_stat, 1)
        t_out, t_sum = conv(double(activate(t_out, t_stat, 5), 2 * t_own, 1, 1), inner_weights[2])
        q_out, q_sum = conv(q_framed, first_weights[0])
        t_stat, q_stat = statistics([(t_sum, t_out.shape[1]), (q_sum, q_out.shape[1])])
        t_act = activate(t_out, t_stat, 6)
        q_act = activate(q_out, q_stat, 0)

        coarse = jnp.einsum(
            "rwc,ck->rkw",
            jnp.concatenate([e_act, s_act, t_act], axis=2),
            jnp.concatenate([class_weight] * 3, axis=0),
            preferred_element_type=jnp.float32,
        )
        (before,), (after,) = edges([coarse], [1], size, 3)
        before = jnp.where(position == 0, coarse[:1], before)
        after = jnp.where(position == size - 1, coarse[-1:], after)
        coarse = jnp.concatenate([before, coarse, after], axis=0).transpose(1, 0, 2)
        wide = jnp.einsum(
            "krw,wv->krv",
            coarse,
            col_matrix(coarse.shape[2]),
            precision=lax.Precision.HIGHEST,
            preferred_element_type=jnp.float32,
        )
        grown = double_rows(wide, 1)[:, 1:-1]
        scores = (
            jnp.einsum("rwc,ck->krw", q_act, class_weight, preferred_element_type=jnp.float32)
            + grown
            + class_bias[:, None, None]
        )
        log_total = jnp.log(jnp.sum(jnp.exp(scores), axis=0))
        label_map = labels[0]
        classes = jnp.arange(scores.shape[0], dtype=jnp.int32)[:, None, None]
        picked = jnp.sum(jnp.where(classes == label_map[None], scores, 0.0), axis=0)
        usable = label_map != 255
        local_total = jnp.sum(jnp.where(usable, log_total - picked, 0.0))
        local_count = jnp.sum(usable.astype(jnp.float32))
        lane = lax.broadcasted_iota(jnp.int32, (8, 128), 1)
        slab = jnp.where(lane == 0, local_total, jnp.where(lane == 1, local_count, 0.0))
        sums = exchange(slab, shape, ("rows",), 0).sum(axis=0)
        sums = exchange(sums, shape, ("batch",), 1)[:, 0].sum(axis=0)
        mean_loss = sums[0] / jnp.maximum(sums[1], 1.0)
        return (scores.astype(jnp.bfloat16)[None], mean_loss)

    return per_device


def solution(mesh):
    in_specs = (
        P("batch", "rows", None, None),
        P("batch", "rows", None, None),
        P("batch", "rows", None, None),
        P("batch", "rows", None, None),
        P("batch", "rows", None),
        P(),
        P(),
        P(),
        P(),
        P(),
        P(),
    )
    out_specs = (P("batch", None, "rows", None), P())
    return jax.shard_map(
        make_per_device(dict(mesh.shape)),
        mesh=mesh,
        in_specs=in_specs,
        out_specs=out_specs,
        check_vma=False,
    )
```

profile of v0, /device:TPU:0, one launch (start us, length us, event | category | flops | bytes accessed | tf_op | source)
XLA Modules:
  0.0 162.3 jit_solution(16644040151989144967)
XLA Ops:
  1.7 2.1 %slice_bitcast_fusion.4 = (bf16[3,3,128,128]{3,2,1,0:T(8,128)(2,1)}, bf16[3,3,128,128]{3,2,1,0:T(8,128)(2,1)}, bf16[3,3,128,128]{3,2,1,0:T(8,128)(2,1)}) fusion(bf16[3,3,3,128,128]{4,3,2,1,0:T(8,128)(2,1)} %param.21), kind=kLoop, calls=%fused_computation.52 | loop fusion | bytes 1769472 | tf_op jit(solution)/shard_map/squeeze | solution.py:311
  3.8 29.9 %shard_map.158 = (bf16[1,512,256]{2,1,0:T(8,128)(2,1)}, bf16[1,256,256]{2,1,0:T(8,128)(2,1)}, bf16[2,128,256]{2,1,0:T(8,128)(2,1)}, bf16[3,64,256]{2,1,0:T(8,128...) custom-call(bf16[16,512,256]{2,1,0:T(8,128)(2,1)} %bitcast.195, ...), custom_call_target="tpu_custom_call" | custom-call | tf_op jit(solution)/shard_map/pallas_call | solution.py:193
  33.7 1.8 %pad_maximum_fusion.7.x_ref = bf16[8,64,256]{2,1,0:T(8,128)(2,1)} fusion(bf16[3,64,256]{2,1,0:T(8,128)(2,1)} %get-tuple-element.30, bf16[2,64,256]{2,1,0:T(8,128)(2,1)S(1)} %bitcast.204, bf16[3,64,256]{2,1,0:T(8,128)(2,1)} %get-tuple-element.29), kind=kLoop, calls=%fused_computation.56 | loop fusion | flops 262144 | bytes 524288 | tf_op jit(solution)/shard_map/concatenate | solution.py:297
  35.5 1.9 %pad_maximum_fusion.5.x_ref = bf16[8,128,256]{2,1,0:T(8,128)(2,1)} fusion(bf16[2,128,256]{2,1,0:T(8,128)(2,1)} %get-tuple-element.34, bf16[4,128,256]{2,1,0:T(8,128)(2,1)S(1)} %bitcast.201, bf16[2,128,256]{2,1,0:T(8,128)(2,1)} %get-tuple-element.33), kind=kLoop, calls=%fused_computation.36 | loop fusion | flops 524288 | bytes 1048576 | tf_op jit(solution)/shard_map/concatenate | solution.py:297
  37.4 2.2 %pad_maximum_fusion.1.x_ref = bf16[10,256,256]{2,1,0:T(8,128)(2,1)} fusion(bf16[1,256,256]{2,1,0:T(8,128)(2,1)} %get-tuple-element.41, bf16[8,256,256]{2,1,0:T(8,128)(2,1)S(1)} %bitcast.198, bf16[1,256,256]{2,1,0:T(8,128)(2,1)} %get-tuple-element.40), kind=kLoop, calls=%fused_computation.9 | loop fusion | flops 1310720 | bytes 2621440 | tf_op jit(solution)/shard_map/concatenate | solution.py:297
  39.6 1.4 slice_bitcast_fusion
  41.0 2.8 %shard_map.161 = (f32[6,128,128]{2,1,0:T(8,128)}, f32[6,2,128]{2,1,0:T(2,128)}) custom-call(bf16[8,128,256]{2,1,0:T(8,128)(2,1)} %pad_maximum_fusion.5.x_ref, bf16[3,3,256,128]{3,2,1,0:T(8,128)(2,1)} %get-tuple-element.93.w_ref), custom_call_target="tpu_custom_call" | custom-call | flops 452984832 | bytes 917504 | tf_op jit(solution)/shard_map/pallas_call | solution.py:104
  44.6 4.5 %shard_map.165 = (f32[8,256,128]{2,1,0:T(8,128)}, f32[8,2,128]{2,1,0:T(2,128)}) custom-call(bf16[10,256,256]{2,1,0:T(8,128)(2,1)} %pad_maximum_fusion.1.x_ref, bf16[3,3,256,128]{3,2,1,0:T(8,128)(2,1)} %get-tuple-element.90.w_ref), custom_call_target="tpu_custom_call" | custom-call | flops 1207959552 | bytes 2359296 | tf_op jit(solution)/shard_map/pallas_call | solution.py:104
  49.1 2.4 %shard_map.160 = (f32[6,64,128]{2,1,0:T(8,128)}, f32[6,2,128]{2,1,0:T(2,128)}) custom-call(bf16[8,64,256]{2,1,0:T(8,128)(2,1)} %pad_maximum_fusion.7.x_ref, bf16[3,3,256,128]{3,2,1,0:T(8,128)(2,1)} %get-tuple-element.91.w_ref), custom_call_target="tpu_custom_call" | custom-call | flops 226492416 | bytes 458752 | tf_op jit(solution)/shard_map/pallas_call | solution.py:104
  55.0 9.7 %shard_map.162 = f32[8,8,128]{2,1,0:T(8,128)} custom-call(f32[8,128]{1,0:T(8,128)} %stack.87.x_ref), custom_call_target="tpu_custom_call" | custom-call | tf_op jit(solution)/shard_map/pallas_call | solution.py:57
  70.4 2.4 %shard_map.163 = (f32[6,128,128]{2,1,0:T(8,128)}, f32[6,2,128]{2,1,0:T(2,128)}) custom-call(bf16[8,128,128]{2,1,0:T(8,128)(2,1)} %slice_select_fusion.x_ref, bf16[3,3,128,128]{3,2,1,0:T(8,128)(2,1)} %get-tuple-element.95.w_ref), custom_call_target="tpu_custom_call" | custom-call | flops 226492416 | bytes 655360 | tf_op jit(solution)/shard_map/pallas_call | solution.py:104
  75.9 3.4 %shard_map.164 = (f32[8,256,128]{2,1,0:T(8,128)}, f32[8,2,128]{2,1,0:T(2,128)}) custom-call(bf16[10,256,128]{2,1,0:T(8,128)(2,1)} %bitcast_select_fusion.1.x_ref, bf16[3,3,128,128]{3,2,1,0:T(8,128)(2,1)} %get-tuple-element.96.w_ref), custom_call_target="tpu_custom_call" | custom-call | flops 603979776 | bytes 1703936 | tf_op jit(solution)/shard_map/pallas_call | solution.py:104
  81.2 7.8 %shard_map.166 = f32[8,8,128]{2,1,0:T(8,128)} custom-call(f32[8,128]{1,0:T(8,128)} %stack.98.x_ref), custom_call_target="tpu_custom_call" | custom-call | tf_op jit(solution)/shard_map/pallas_call | solution.py:57
  94.2 3.4 %shard_map.167 = (f32[8,256,128]{2,1,0:T(8,128)}, f32[8,2,128]{2,1,0:T(2,128)}) custom-call(bf16[10,256,128]{2,1,0:T(8,128)(2,1)} %bitcast_select_fusion.x_ref, bf16[3,3,128,128]{3,2,1,0:T(8,128)(2,1)} %get-tuple-element.94.w_ref), custom_call_target="tpu_custom_call" | custom-call | flops 603979776 | bytes 1703936 | tf_op jit(solution)/shard_map/pallas_call | solution.py:104
  98.9 4.0 %pad_maximum_fusion.x_ref = bf16[18,512,256]{2,1,0:T(8,128)(2,1)} fusion(bf16[1,512,256]{2,1,0:T(8,128)(2,1)S(1)} %copy-done.10, bf16[16,512,256]{2,1,0:T(8,128)(2,1)} %bitcast.196, bf16[1,512,256]{2,1,0:T(8,128)(2,1)S(1)} %copy-done.9), kind=kLoop, calls=%fused_computation | loop fusion | flops 4718592 | bytes 9437184 | tf_op jit(solution)/shard_map/concatenate | solution.py:297
  102.9 12.4 %shard_map.159 = (f32[16,512,128]{2,1,0:T(8,128)}, f32[16,2,128]{2,1,0:T(2,128)}) custom-call(bf16[18,512,256]{2,1,0:T(8,128)(2,1)} %pad_maximum_fusion.x_ref, bf16[3,3,256,128]{3,2,1,0:T(8,128)(2,1)} %get-tuple-element.92.w_ref), custom_call_target="tpu_custom_call" | custom-call | flops 4831838208 | bytes 8912896 | tf_op jit(solution)/shard_map/pallas_call | solution.py:104
  117.3 7.8 %shard_map.168 = f32[8,8,128]{2,1,0:T(8,128)} custom-call(f32[8,128]{1,0:T(8,128)} %stack.104.x_ref), custom_call_target="tpu_custom_call" | custom-call | tf_op jit(solution)/shard_map/pallas_call | solution.py:57
  128.0 1.4 maximum_convert_fusion.10
  130.0 1.4 fusion.10.refs_0_
  131.4 5.0 %shard_map.169 = (f32[1,19,256]{2,1,0:T(8,128)}, f32[1,19,256]{2,1,0:T(8,128)}) custom-call(f32[8,19,256]{2,1,0:T(8,128)} %fusion.10.refs_0_), custom_call_target="tpu_custom_call" | custom-call | tf_op jit(solution)/shard_map/pallas_call | solution.py:193
  137.3 1.7 %fusion.17 = f32[19,10,512]{2,0,1:T(8,128)S(1)} fusion(f32[256,512,1]{1,0,2:T(8,128)S(1)} %copy-done.5, f32[1,19,256]{2,1,0:T(8,128)S(1)} %get-tuple-element.107, f32[8,19,256]{2,1,0:T(8,128)} %fusion.10.refs_0_, f32[1,19,256]{2,1,0:T(8,128)S(1)} %get-tuple-element.106), kind=kOutput, calls=%fused_computation.58 | convolution fusion | flops 298941440 | bytes 1107968 | tf_op jit(solution)/shard_map/krw,wv->krv/dot_general | solution.py:327
  143.3 8.1 %shard_map.170 = f32[8,8,128]{2,1,0:T(8,128)} custom-call(f32[8,128]{1,0:T(8,128)} %broadcast_select_fusion.x_ref), custom_call_target="tpu_custom_call" | custom-call | tf_op jit(solution)/shard_map/pallas_call | solution.py:57
  151.4 1.4 reduce_sum.578.x_ref
  152.8 5.0 %shard_map.171 = f32[4,8,128]{2,1,0:T(8,128)} custom-call(f32[8,128]{1,0:T(8,128)} %reduce_sum.578.x_ref), custom_call_target="tpu_custom_call" | custom-call | tf_op jit(solution)/shard_map/pallas_call | solution.py:57
  (206 shorter events, 34.7 us)
Async XLA Ops:
  3.7 29.9 %copy-start.8 = (bf16[1,2,64,256]{3,2,1,0:T(8,128)(2,1)S(1)}, bf16[1,2,64,256]{3,2,1,0:T(8,128)(2,1)}, u32[]{:S(2)}) copy-start(bf16[1,2,64,256]{3,2,1,0:T(8,128)(2,1)} %param.18) | copy-start | bytes 196612
  3.8 31.8 %copy-start.4 = (bf16[1,4,128,256]{3,2,1,0:T(8,128)(2,1)S(1)}, bf16[1,4,128,256]{3,2,1,0:T(8,128)(2,1)}, u32[]{:S(2)}) copy-start(bf16[1,4,128,256]{3,2,1,0:T(8,128)(2,1)} %param.17) | copy-start | bytes 786436
  3.8 33.6 %copy-start = (bf16[1,8,256,256]{3,2,1,0:T(8,128)(2,1)S(1)}, bf16[1,8,256,256]{3,2,1,0:T(8,128)(2,1)}, u32[]{:S(2)}) copy-start(bf16[1,8,256,256]{3,2,1,0:T(8,128)(2,1)} %param.16) | copy-start | bytes 3145732
  33.7 5.9 %copy-start.1 = (bf16[4,3,3,256,128]{4,3,2,1,0:T(8,128)(2,1)S(1)}, bf16[4,3,3,256,128]{4,3,2,1,0:T(8,128)(2,1)}, u32[]{:S(2)}) copy-start(bf16[4,3,3,256,128]{4,3,2,1,0:T(8,128)(2,1)} %param.20) | copy-start | bytes 7077892
  44.6 23.1 %copy-start.14 = (f32[7,128]{1,0:T(8,128)S(1)}, f32[7,128]{1,0:T(8,128)}, u32[]{:S(2)}) copy-start(f32[7,128]{1,0:T(8,128)} %param.22) | copy-start | bytes 10756
  44.6 24.2 %copy-start.6 = (f32[6,128,128]{2,1,0:T(8,128)S(1)}, f32[6,128,128]{2,1,0:T(8,128)}, u32[]{:S(2)}) copy-start(f32[6,128,128]{2,1,0:T(8,128)} %get-tuple-element.38) | copy-start | bytes 1179652
  49.1 19.8 %copy-start.13 = (bf16[64,128,1]{1,0,2:T(8,128)(2,1)S(1)}, bf16[64,128,1]{1,0,2:T(8,128)(2,1)}, u32[]{:S(2)}) copy-start(bf16[64,128,1]{1,0,2:T(8,128)(2,1)} %constant.153) | copy-start | bytes 49156
  65.8 8.2 %copy-start.11 = (bf16[128,256,1]{1,0,2:T(8,128)(2,1)S(1)}, bf16[128,256,1]{1,0,2:T(8,128)(2,1)}, u32[]{:S(2)}) copy-start(bf16[128,256,1]{1,0,2:T(8,128)(2,1)} %constant.154) | copy-start | bytes 196612
  74.9 16.6 %copy-start.7 = (f32[6,128,128]{2,1,0:T(8,128)S(1)}, f32[6,128,128]{2,1,0:T(8,128)}, u32[]{:S(2)}) copy-start(f32[6,128,128]{2,1,0:T(8,128)} %get-tuple-element.36) | copy-start | bytes 1179652
  92.9 6.0 %copy-start.9 = (bf16[1,512,256]{2,1,0:T(8,128)(2,1)S(1)}, bf16[1,512,256]{2,1,0:T(8,128)(2,1)}, u32[]{:S(2)}) copy-start(bf16[1,512,256]{2,1,0:T(8,128)(2,1)} %get-tuple-element.26) | copy-start | bytes 786436
  92.9 6.0 %copy-start.10 = (bf16[1,512,256]{2,1,0:T(8,128)(2,1)S(1)}, bf16[1,512,256]{2,1,0:T(8,128)(2,1)}, u32[]{:S(2)}) copy-start(bf16[1,512,256]{2,1,0:T(8,128)(2,1)} %get-tuple-element.27) | copy-start | bytes 786436
  115.3 14.3 %copy-start.2 = (f32[8,256,128]{2,1,0:T(8,128)S(1)}, f32[8,256,128]{2,1,0:T(8,128)}, u32[]{:S(2)}) copy-start(f32[8,256,128]{2,1,0:T(8,128)} %get-tuple-element.46) | copy-start | bytes 3145732
  115.3 14.3 %copy-start.3 = (f32[8,256,128]{2,1,0:T(8,128)S(1)}, f32[8,256,128]{2,1,0:T(8,128)}, u32[]{:S(2)}) copy-start(f32[8,256,128]{2,1,0:T(8,128)} %get-tuple-element.47) | copy-start | bytes 3145732
  126.1 3.9 %copy-start.15 = (bf16[128,19]{0,1:T(8,128)(2,1)S(1)}, bf16[128,19]{0,1:T(8,128)(2,1)}, u32[]{:S(2)}) copy-start(bf16[128,19]{0,1:T(8,128)(2,1)} %param.24) | copy-start | bytes 14596
  129.6 7.6 %copy-start.5 = (f32[256,512,1]{1,0,2:T(8,128)S(1)}, f32[256,512,1]{1,0,2:T(8,128)}, u32[]{:S(2)}) copy-start(f32[256,512,1]{1,0,2:T(8,128)} %constant.155) | copy-start | bytes 1572868
  137.2 2.0 %copy-start.12 = (s32[1,16,512]{2,1,0:T(8,128)S(1)}, s32[1,16,512]{2,1,0:T(8,128)}, u32[]{:S(2)}) copy-start(s32[1,16,512]{2,1,0:T(8,128)} %param.19) | copy-start | bytes 98308
  137.2 2.0 %copy-start.16 = (f32[19]{0:T(128)S(1)}, f32[19]{0:T(128)}, u32[]{:S(2)}) copy-start(f32[19]{0:T(128)} %param.25) | copy-start | bytes 232
  137.2 2.3 %copy-start.17 = (f32[16,512,128]{2,1,0:T(8,128)S(1)}, f32[16,512,128]{2,1,0:T(8,128)}, u32[]{:S(2)}) copy-start(f32[16,512,128]{2,1,0:T(8,128)} %get-tuple-element.28) | copy-start | bytes 12582916
where the time goes:
time: 164 us; the launch traced here: 162 us
  Pallas kernels  104 us (63%)
  other arithmetic  31.2 us (19%)
  local copies, waits for them, and re-layouts  17.4 us (11%)
  matrix products  5.34 us (3%)
  between operations  3.99 us (2%)
    pallas_call x5, Pallas kernels, exchange(): pl.pallas_call(functools.partial(exchange_kernel, shape, axes), out_shape...  38.3 us
    pallas_call x2, Pallas kernels, edges(): pl.pallas_call(functools.partial(edges_kernel, size, tuple(widths)), out_...  34.9 us
    pallas_call x7, Pallas kernels, conv(): pl.pallas_call(functools.partial(conv_kernel, rows), grid=(count // rows,...  31.2 us
    concatenate x4, other arithmetic, per_device(): jnp.concatenate([x, band, z], axis=0)  9.91 us
    reduce_sum x7, other arithmetic, statistics(): slab += [sums, rows[:, 1].sum(axis=0) + strays]  5.59 us

commit v1 on v0

v1 whole, which is shorter than its diff:
```python
import functools

import jax
import jax.numpy as jnp
from jax import lax
from jax.experimental import pallas as pl
from jax.experimental.pallas import tpu as pltpu
from jax.sharding import PartitionSpec as P

GROUPS = 32
NORM_FLOOR = 0.05
IGNORED = 255
Q_CHUNKS = 8
E_CHUNKS = 2
MESH = pl.DeviceIdType.MESH
F32 = jnp.float32
BF16 = jnp.bfloat16


def group_fold(x):
    width = x.shape[-1]
    lane = lax.broadcasted_iota(jnp.int32, x.shape, x.ndim - 1)
    step = 1
    while step < width // GROUPS:
        ahead = pltpu.roll(x, width - step, x.ndim - 1)
        behind = pltpu.roll(x, step, x.ndim - 1)
        x = x + jnp.where(lax.rem(lane, 2 * step) < step, ahead, behind)
        step *= 2
    return x


def doubling(rows, cols, source_axis):
    source = lax.broadcasted_iota(jnp.int32, (rows, cols), source_axis)
    target = lax.broadcasted_iota(jnp.int32, (rows, cols), 1 - source_axis)
    count = (rows, cols)[source_axis]
    near = lax.div(target, 2)
    far = jnp.clip(near + 2 * lax.rem(target, 2) - 1, 0, count - 1)
    return (
        0.75 * (source == near).astype(F32) + 0.25 * (source == far).astype(F32)
    ).astype(BF16)


def conv_block(x_ref, flat_ref, start, rows):
    cols, depth = x_ref.shape[1:]
    width = flat_ref.shape[1] // 3
    lhs = jnp.concatenate(
        [
            x_ref[pl.ds(start + down, rows)].reshape(rows * cols, depth)
            for down in range(3)
        ],
        axis=1,
    )
    taps = jnp.dot(lhs, flat_ref[...], preferred_element_type=F32)
    col = lax.rem(lax.broadcasted_iota(jnp.int32, (rows * cols, width), 0), cols)
    left = jnp.where(col == 0, 0.0, pltpu.roll(taps[:, :width], 1, 0))
    right = jnp.where(col == cols - 1, 0.0, pltpu.roll(taps[:, 2 * width :], rows * cols - 1, 0))
    return (taps[:, width : 2 * width] + left + right).reshape(rows, cols, width)


def conv_to(x_ref, flat_ref, y_ref, stat_ref, start, rows, offset):
    y = conv_block(x_ref, flat_ref, start, rows)
    cols = y.shape[1]
    y_ref[pl.ds(start + offset, rows)] = y
    sums = jnp.sum(y, axis=1, keepdims=True)
    centred = y - sums / cols
    stat_ref[pl.ds(start, rows), 0:1] = sums
    stat_ref[pl.ds(start, rows), 1:2] = jnp.sum(centred * centred, axis=1, keepdims=True)


def head_kernel(
    shape,
    q, e, s, t, labels, first_w, inner_w, gain, shift, class_w, bias,
    out, loss_out,
    q_in, e_in, s_in, t_in, w_q, w_e, w_s, w_t, w_i,
    q_y, e_y, s_y, t_y, s_grown, s_y2, t_grown, t_y2, t_grown2, t_y3,
    q_stat, e_stat, s_stat, t_stat, s_stat2, t_stat2, t_stat3,
    slab, slabs, class_f, class_pad, up_t, up_s, coarse, wide, scores_q, loss_slab, loss_slabs,
    local_sem, edge_send, edge_recv, slab_send, slab_recv, loss_send, loss_recv,
):
    size, images = shape["rows"], shape["batch"]
    total = size * images
    me, image = lax.axis_index("rows"), lax.axis_index("batch")
    flat = image * size + me
    width = q_y.shape[2]
    classes = class_w.shape[0]

    def device_at(distance):
        number = lax.rem(flat + distance, total)
        return {"batch": lax.div(number, size), "rows": lax.rem(number, size)}

    barrier = pltpu.get_barrier_semaphore()

    def greet(distance, carry):
        pl.semaphore_signal(
            barrier, inc=1, device_id=device_at(distance), device_id_type=MESH
        )
        return carry

    lax.fori_loop(1, total, greet, 0)

    fetched = []

    def fetch(source, target):
        copy = pltpu.make_async_copy(source, target, local_sem.at[len(fetched)])
        copy.start()
        fetched.append(copy)
        return copy

    def fetch_weights(source, target):
        depth = source.shape[2]
        return [
            fetch(
                source.at[down, across],
                target.at[down * depth : (down + 1) * depth, across * width : (across + 1) * width],
            )
            for down in range(3)
            for across in range(3)
        ]

    def settle(copies):
        for copy in copies:
            copy.wait()

    q_rows, q_cols = q.shape[:2]
    e_rows, s_rows, t_rows = e.shape[0], s.shape[0], t.shape[0]
    got_q = fetch_weights(first_w.at[0], w_q) + [fetch(q, q_in.at[1 : q_rows + 1])]
    got_t = fetch_weights(first_w.at[3], w_t) + [fetch(t, t_in.at[1 : t_rows + 1])]
    got_s = fetch_weights(first_w.at[2], w_s) + [fetch(s, s_in.at[1 : s_rows + 1])]
    got_i = [c for i in range(3) for c in fetch_weights(inner_w.at[i], w_i.at[i])]
    got_e = fetch_weights(first_w.at[1], w_e) + [fetch(e, e_in.at[1 : e_rows + 1])]

    def exists(offset):
        return me + offset < size if offset > 0 else me + offset >= 0

    def neighbour(offset):
        return {"rows": lax.rem(me + offset + size, size)}

    sent = []

    def edge(source_of, target_of, number, offset):
        own = source_of.shape[0]
        return pltpu.make_async_remote_copy(
            src_ref=source_of,
            dst_ref=target_of,
            send_sem=edge_send.at[number],
            recv_sem=edge_recv.at[number],
            device_id=neighbour(offset),
            device_id_type=MESH,
        )

    def edges(source, first, last, target, before, after, number, part=None):
        def at(ref, row):
            return ref.at[row] if part is None else ref.at[row, part]

        return [
            (edge(at(source, last), at(target, before), number, 1), 1),
            (edge(at(source, first), at(target, after), number + 1, -1), -1),
        ]

    def send(pairs):
        for copy, offset in pairs:
            pl.when(exists(offset))(copy.start)

    def arrive(pairs):
        for copy, offset in pairs:
            pl.when(exists(-offset))(copy.wait_recv)

    def leave(pairs):
        for copy, offset in pairs:
            pl.when(exists(offset))(copy.wait_send)

    def feature_edges(source, target, number, part=None):
        count = source.shape[0]
        return edges(source, 0, count - 1, target, 0, count + 1, number, part)

    def band_edges(field, number):
        count = field.shape[0] - 2
        return edges(field, 1, count, field, 0, count + 1, number)

    t_edges, s_edges = feature_edges(t, t_in, 0), feature_edges(s, s_in, 2)
    t_y_edges, s_y_edges, t_y2_edges = band_edges(t_y, 4), band_edges(s_y, 6), band_edges(t_y2, 8)
    coarse_edges = band_edges(coarse, 10)

    def e_edges(chunk):
        part = pl.ds(pl.multiple_of(chunk * (e.shape[1] // E_CHUNKS), 16), e.shape[1] // E_CHUNKS)
        return feature_edges(e, e_in, 12 + 2 * chunk, part)

    def q_edges(chunk):
        part = pl.ds(pl.multiple_of(chunk * (q_cols // Q_CHUNKS), 16), q_cols // Q_CHUNKS)
        return feature_edges(q, q_in, 12 + 2 * E_CHUNKS + 2 * chunk, part)

    def each_chunk(count, act):
        def step(chunk, carry):
            act(chunk)
            return carry

        lax.fori_loop(0, count, step, 0)

    @pl.when(me == 0)
    def _():
        for field in (q_in, e_in, s_in, t_in):
            field[0] = jnp.zeros(field.shape[1:], BF16)

    @pl.when(me == size - 1)
    def _():
        for field in (q_in, e_in, s_in, t_in):
            field[field.shape[0] - 1] = jnp.zeros(field.shape[1:], BF16)

    slab[...] = jnp.zeros(slab.shape, F32)
    loss_slab[...] = jnp.zeros(loss_slab.shape, F32)
    up_t[...] = doubling(*up_t.shape, 1)
    up_s[...] = doubling(*up_s.shape, 1)
    class_f[...] = jnp.zeros(class_f.shape, F32)
    class_f[0:classes] = class_w[...].astype(F32)
    class_pad[...] = class_f[...].astype(BF16)
    padded = class_f.shape[0]
    spot = lax.broadcasted_iota(jnp.int32, (padded, classes), 0)
    lane = lax.broadcasted_iota(jnp.int32, (padded, classes), 1)
    bias_col = jnp.sum(jnp.where(spot == lane, bias[...], 0.0), axis=1, keepdims=True)

    pl.semaphore_wait(barrier, total - 1)
    send(t_edges)
    send(s_edges)

    def slab_copy(number, distance):
        return pltpu.make_async_remote_copy(
            src_ref=slab.at[number],
            dst_ref=slabs.at[number, me],
            send_sem=slab_send.at[number, distance],
            recv_sem=slab_recv.at[number, distance],
            device_id=neighbour(distance),
            device_id_type=MESH,
        )

    def slab_arrival(number, distance):
        sender = lax.rem(me - distance + size, size)
        return pltpu.make_async_remote_copy(
            src_ref=slab.at[number],
            dst_ref=slabs.at[number, sender],
            send_sem=slab_send.at[number, distance],
            recv_sem=slab_recv.at[number, distance],
            device_id=neighbour(distance),
            device_id_type=MESH,
        )

    def announce(number, fields):
        for place, (stat, cols) in enumerate(fields):
            rows = stat.shape[0]
            sums = stat[:, 0:1]
            channel = jnp.sum(sums, axis=0)
            mean = group_fold(channel) / (rows * cols * (width // GROUPS))
            strays = sums / cols - mean
            squares = jnp.sum(stat[:, 1:2] + cols * (strays * strays), axis=0)
            slab[number, 2 * place : 2 * place + 1] = channel
            slab[number, 2 * place + 1 : 2 * place + 2] = squares
        for distance in range(1, size):
            slab_copy(number, distance).start()
        slabs[number, me] = slab[number]

    def gather(number, counts):
        for distance in range(1, size):
            slab_arrival(number, distance).wait_recv()
        every = slabs[number]
        every = group_fold(every.reshape(size * every.shape[1], width)).reshape(every.shape)
        result = []
        for place, count in enumerate(counts):
            means = every[:, 2 * place : 2 * place + 1] / count
            mean = jnp.sum(means, axis=0) / size
            strays = means - mean
            squares = jnp.sum(
                every[:, 2 * place + 1 : 2 * place + 2] + count * (strays * strays), axis=0
            )
            result.append((mean, squares / (count * size)))
        return result

    def count_of(rows, cols):
        return rows * cols * (width // GROUPS)

    def activation(stat, layer):
        mean, var = stat
        factor = gain[layer : layer + 1] * lax.rsqrt(var + NORM_FLOOR)
        offset = shift[layer : layer + 1]
        return lambda y: jnp.maximum((y - mean) * factor + offset, 0.0).astype(BF16)

    def grow(field, grown, up, act):
        own = field.shape[0] - 2

        @pl.when(me == 0)
        def _():
            field[0] = field[1]

        @pl.when(me == size - 1)
        def _():
            field[own + 1] = field[own]

        lines = jnp.concatenate([act(field[row]) for row in range(own + 2)], axis=1)
        lines = jnp.dot(up[...], lines, preferred_element_type=F32)
        for row in range(own + 1):
            here = lines[:, row * width : (row + 1) * width]
            below = lines[:, (row + 1) * width : (row + 2) * width]
            grown[2 * row] = (0.75 * here + 0.25 * below).astype(BF16)
            grown[2 * row + 1] = (0.25 * here + 0.75 * below).astype(BF16)

        @pl.when(me == 0)
        def _():
            grown[0] = jnp.zeros(grown.shape[1:], BF16)

        @pl.when(me == size - 1)
        def _():
            grown[2 * own + 1] = jnp.zeros(grown.shape[1:], BF16)

    def convolve(x_ref, flat_ref, y_ref, stat_ref, rows, offset):
        count = x_ref.shape[0] - 2

        def step(index, carry):
            conv_to(x_ref, flat_ref, y_ref, stat_ref, index * rows, rows, offset)
            return carry

        lax.fori_loop(0, count // rows, step, 0)

    def rows_within(count, cols):
        return max(r for r in range(1, count + 1) if count % r == 0 and (r == 1 or r * cols <= 1024))

    def q_blocks(first, last, chunk):
        def step(index, carry):
            if chunk is not None:
                send(q_edges(chunk + index - first))
            conv_to(q_in, w_q, q_y, q_stat, 1 + 2 * index, 2, 0)
            return carry

        lax.fori_loop(first, last, step, 0)

    blocks = (q_rows - 2) // 2
    settle(got_q)
    q_blocks(0, 2, None)

    settle(got_t)
    arrive(t_edges)
    conv_to(t_in, w_t, t_y, t_stat, 0, t_rows, 1)
    settle(got_s)
    arrive(s_edges)
    conv_to(s_in, w_s, s_y, s_stat, 0, s_rows, 1)
    announce(0, [(t_stat, t.shape[1]), (s_stat, s.shape[1])])
    send(t_y_edges)
    send(s_y_edges)
    for chunk in range(E_CHUNKS):
        send(e_edges(chunk))
    q_blocks(2, 4, 0)

    t_norm, s_norm = gather(0, [count_of(t_rows, t.shape[1]), count_of(s_rows, s.shape[1])])
    settle(got_i)
    arrive(t_y_edges)
    grow(t_y, t_grown, up_t, activation(t_norm, 3))
    convolve(t_grown, w_i.at[1], t_y2, t_stat2, rows_within(2 * t_rows, 2 * t.shape[1]), 1)
    arrive(s_y_edges)
    grow(s_y, s_grown, up_s, activation(s_norm, 2))
    convolve(s_grown, w_i.at[0], s_y2, s_stat2, rows_within(2 * s_rows, 2 * s.shape[1]), 0)
    announce(1, [(t_stat2, 2 * t.shape[1]), (s_stat2, 2 * s.shape[1])])
    send(t_y2_edges)
    q_blocks(4, 6, 2)
    settle(got_e)
    for chunk in range(E_CHUNKS):
        arrive(e_edges(chunk))
    convolve(e_in, w_e, e_y, e_stat, rows_within(e_rows, e.shape[1]), 0)

    t_norm, s_norm = gather(
        1, [count_of(2 * t_rows, 2 * t.shape[1]), count_of(2 * s_rows, 2 * s.shape[1])]
    )
    each_chunk(Q_CHUNKS - 4, lambda chunk: send(q_edges(chunk + 4)))
    arrive(t_y2_edges)
    grow(t_y2, t_grown2, up_s, activation(t_norm, 5))
    convolve(t_grown2, w_i.at[2], t_y3, t_stat3, rows_within(4 * t_rows, 4 * t.shape[1]), 0)
    announce(2, [(t_stat3, 4 * t.shape[1]), (e_stat, e.shape[1])])
    q_blocks(6, blocks, None)
    each_chunk(Q_CHUNKS, lambda chunk: arrive(q_edges(chunk)))

    def border(index, carry):
        conv_to(q_in, w_q, q_y, q_stat, index * (q_rows - 1), 1, 0)
        return carry

    lax.fori_loop(0, 2, border, 0)
    announce(3, [(q_stat, q_cols)])

    t_norm, e_norm = gather(
        2, [count_of(4 * t_rows, 4 * t.shape[1]), count_of(e_rows, e.shape[1])]
    )
    e_act, s_act, t_act = activation(e_norm, 1), activation(s_norm, 4), activation(t_norm, 6)
    weight = class_pad[...]
    weights = jnp.concatenate([weight] * 3, axis=1)
    across = (((1,), (1,)), ((), ()))

    def project(row, carry):
        lines = jnp.concatenate([e_act(e_y[row]), s_act(s_y2[row]), t_act(t_y3[row])], axis=1)
        coarse[row + 1] = lax.dot_general(weights, lines, across, preferred_element_type=F32)
        return carry

    lax.fori_loop(0, e_rows, project, 0)
    send(coarse_edges)

    (q_norm,) = gather(3, [count_of(q_rows, q_cols)])
    q_act = activation(q_norm, 0)

    def score(row, carry):
        scores_q[row] = (
            lax.dot_general(weight, q_act(q_y[row]), across, preferred_element_type=F32) + bias_col
        )
        return carry

    lax.fori_loop(0, q_rows, score, 0)
    up_cols = doubling(e.shape[1], q_cols, 0)
    arrive(coarse_edges)

    @pl.when(me == 0)
    def _():
        coarse[0] = coarse[1]

    @pl.when(me == size - 1)
    def _():
        coarse[e_rows + 1] = coarse[e_rows]

    lines = coarse[...].reshape((e_rows + 2) * padded, e.shape[1])
    high = lines.astype(BF16)
    low = (lines - high.astype(F32)).astype(BF16)
    lines = jnp.dot(high, up_cols, preferred_element_type=F32) + jnp.dot(
        low, up_cols, preferred_element_type=F32
    )
    wide[...] = lines.reshape(wide.shape)
    kind = lax.broadcasted_iota(jnp.int32, (padded, q_cols), 0)

    def finish(row, grown):
        scores = scores_q[row] + grown
        out[row] = scores.astype(BF16)
        powers = jnp.where(kind < classes, jnp.exp(scores), 0.0)
        log_total = jnp.log(jnp.sum(powers, axis=0, keepdims=True))
        label = labels[pl.ds(row, 1), :]
        picked = jnp.sum(jnp.where(kind == label, scores, 0.0), axis=0, keepdims=True)
        usable = label != IGNORED
        return jnp.where(usable, log_total - picked, 0.0), usable.astype(F32)

    def pair(index, carry):
        here = wide[index + 1]
        upper = finish(2 * index, 0.25 * wide[index] + 0.75 * here)
        lower = finish(2 * index + 1, 0.75 * here + 0.25 * wide[index + 2])
        return carry[0] + upper[0] + lower[0], carry[1] + upper[1] + lower[1]

    zero = jnp.zeros((1, q_cols), F32)
    sums = lax.fori_loop(0, e_rows, pair, (zero, zero))
    for place, line in enumerate(sums):
        loss_slab[place : place + 1] = sum(
            line[:, k * width : (k + 1) * width] for k in range(q_cols // width)
        )

    def loss_copy(distance, sender):
        return pltpu.make_async_remote_copy(
            src_ref=loss_slab,
            dst_ref=loss_slabs.at[sender],
            send_sem=loss_send.at[distance],
            recv_sem=loss_recv.at[distance],
            device_id=device_at(distance),
            device_id_type=MESH,
        )

    def loss_go(distance, carry):
        loss_copy(distance, flat).start()
        return carry

    def loss_come(distance, carry):
        loss_copy(distance, lax.rem(flat - distance + total, total)).wait_recv()
        return carry

    def loss_gone(distance, carry):
        loss_copy(distance, flat).wait_send()
        return carry

    lax.fori_loop(1, total, loss_go, 0)
    loss_slabs[flat] = loss_slab[...]
    for pairs in (t_edges, s_edges, t_y_edges, s_y_edges, t_y2_edges, coarse_edges):
        leave(pairs)
    for chunk in range(E_CHUNKS):
        leave(e_edges(chunk))
    each_chunk(Q_CHUNKS, lambda chunk: leave(q_edges(chunk)))
    for number in range(4):
        for distance in range(1, size):
            slab_copy(number, distance).wait_send()
    lax.fori_loop(1, total, loss_come, 0)
    ends = jnp.sum(jnp.sum(loss_slabs[...], axis=0), axis=1, keepdims=True)
    loss_out[...] = jnp.broadcast_to(ends[0:1] / jnp.maximum(ends[1:2], 1.0), loss_out.shape)
    lax.fori_loop(1, total, loss_gone, 0)


def make_per_device(shape):
    def per_device(
        feat_quarter,
        feat_eighth,
        feat_sixteenth,
        feat_thirty,
        labels,
        first_weights,
        inner_weights,
        norm_gain,
        norm_shift,
        class_weight,
        class_bias,
    ):
        q, e, s, t = feat_quarter[0], feat_eighth[0], feat_sixteenth[0], feat_thirty[0]
        size = shape["rows"]
        total = size * shape["batch"]
        depth, width = first_weights.shape[3:]
        classes = class_weight.shape[1]
        padded = -(-classes // 8) * 8
        (q_rows, q_cols), (e_rows, e_cols) = q.shape[:2], e.shape[:2]
        (s_rows, s_cols), (t_rows, t_cols) = s.shape[:2], t.shape[:2]

        def framed(rows, cols, channels, kind=BF16):
            return pltpu.VMEM((rows + 2, cols, channels), kind)

        def field(rows, cols):
            return pltpu.VMEM((rows, cols, width), F32)

        def stat(rows):
            return pltpu.VMEM((rows, 8, width), F32)

        edges = 12 + 2 * E_CHUNKS + 2 * Q_CHUNKS
        scratch = [
            framed(q_rows, q_cols, depth),
            framed(e_rows, e_cols, depth),
            framed(s_rows, s_cols, depth),
            framed(t_rows, t_cols, depth),
            *[pltpu.VMEM((3 * depth, 3 * width), BF16)] * 4,
            pltpu.VMEM((3, 3 * width, 3 * width), BF16),
            field(q_rows, q_cols),
            field(e_rows, e_cols),
            framed(s_rows, s_cols, width, F32),
            framed(t_rows, t_cols, width, F32),
            framed(2 * s_rows, 2 * s_cols, width),
            field(2 * s_rows, 2 * s_cols),
            framed(2 * t_rows, 2 * t_cols, width),
            framed(2 * t_rows, 2 * t_cols, width, F32),
            framed(4 * t_rows, 4 * t_cols, width),
            field(4 * t_rows, 4 * t_cols),
            stat(q_rows),
            stat(e_rows),
            stat(s_rows),
            stat(t_rows),
            stat(2 * s_rows),
            stat(2 * t_rows),
            stat(4 * t_rows),
            pltpu.VMEM((4, 8, width), F32),
            pltpu.VMEM((4, size, 8, width), F32),
            pltpu.VMEM((padded, width), F32),
            pltpu.VMEM((padded, width), BF16),
            pltpu.VMEM((2 * t_cols, t_cols), BF16),
            pltpu.VMEM((2 * s_cols, s_cols), BF16),
            framed(e_rows, padded, e_cols, F32),
            framed(e_rows, padded, q_cols, F32),
            pltpu.VMEM((q_rows, padded, q_cols), F32),
            pltpu.VMEM((8, width), F32),
            pltpu.VMEM((total, 8, width), F32),
            pltpu.SemaphoreType.DMA((80,)),
            pltpu.SemaphoreType.DMA((edges,)),
            pltpu.SemaphoreType.DMA((edges,)),
            pltpu.SemaphoreType.DMA((4, size)),
            pltpu.SemaphoreType.DMA((4, size)),
            pltpu.SemaphoreType.DMA((total,)),
            pltpu.SemaphoreType.DMA((total,)),
        ]
        held = pl.BlockSpec(memory_space=pltpu.VMEM)
        away = pl.BlockSpec(memory_space=pl.ANY)
        scores, loss = pl.pallas_call(
            functools.partial(head_kernel, shape),
            out_shape=(
                jax.ShapeDtypeStruct((q_rows, padded, q_cols), BF16),
                jax.ShapeDtypeStruct((8, width), F32),
            ),
            in_specs=[away] * 4 + [held] + [away] * 2 + [held] * 4,
            out_specs=(held, held),
            scratch_shapes=scratch,
            compiler_params=pltpu.CompilerParams(
                collective_id=0, has_side_effects=True, vmem_limit_bytes=60 << 20
            ),
        )(
            q, e, s, t, labels[0], first_weights, inner_weights, norm_gain, norm_shift,
            class_weight.T, class_bias[None],
        )
        return (scores[:, :classes].transpose(1, 0, 2)[None], loss[0, 0])

    return per_device


def solution(mesh):
    in_specs = (
        P("batch", "rows", None, None),
        P("batch", "rows", None, None),
        P("batch", "rows", None, None),
        P("batch", "rows", None, None),
        P("batch", "rows", None),
        P(),
        P(),
        P(),
        P(),
        P(),
        P(),
    )
    out_specs = (P("batch", None, "rows", None), P())
    return jax.shard_map(
        make_per_device(dict(mesh.shape)),
        mesh=mesh,
        in_specs=in_specs,
        out_specs=out_specs,
        check_vma=False,
    )
```

time: 164 us -> 62.6 us (0.38)
  Pallas kernels: 104 us -> 58.7 us
  other arithmetic: 31.2 us -> 0 us
  local copies, waits for them, and re-layouts: 17.4 us -> 3.02 us
  matrix products: 5.34 us -> 0 us
  between operations: 3.99 us -> 0.65 us
    pallas_call x14 -> x1, Pallas kernels: 104 us -> 58.7 us  [per_device(): pl.pallas_call(functools.partial(head_kernel, shape), out_shape=(jax.Shap...]
    reduce_sum x37 -> x0, other arithmetic: 12.1 us -> none  [the longest x7 5.59 us: statistics(): slab += [sums, rows[:, 1].sum(axis=0) + strays]]
    concatenate x4 -> x0, other arithmetic: 9.91 us -> none  [per_device(): jnp.concatenate([x, band, z], axis=0)]
    select_n x6 -> x0, other arithmetic: 5.39 us -> none  [the longest x3 2.7 us: double(): return jnp.where(inside, grown, jnp.zeros_like(grown))]
    dot_general x6 -> x0, matrix products: 5.34 us -> none  [the longest x1 1.67 us: per_device(): jnp.einsum('krw,wv->krv', coarse, col_matrix(coarse.shape[2]), precision=...]
    squeeze x2 -> x0, local copies, waits for them, and re-layouts: 3.49 us -> none  [the longest x1 2.05 us: per_device(): inner_weights[2]]
    pallas_call x3 -> x0, local copies, waits for them, and re-layouts: 2.98 us -> none  [exchange(): pl.pallas_call(functools.partial(exchange_kernel, shape, axes), out_shape...]
    convert_element_type x5 -> x0, other arithmetic: 2.92 us -> none  [activate(): return jnp.maximum((y - spread(stat[0], width)) * factor + norm_shift[lay...]
where the time goes in v1:
time: 62.6 us; the launch traced here: 62.4 us
  Pallas kernels  58.7 us (94%)
  local copies, waits for them, and re-layouts  3.02 us (5%)
  between operations  0.65 us (1%)
    pallas_call x1, Pallas kernels, per_device(): pl.pallas_call(functools.partial(head_kernel, shape), out_shape=(jax.Shap...  58.7 us

profile of v1, /device:TPU:0, one launch (start us, length us, event | category | flops | bytes accessed | tf_op | source)
XLA Modules:
  0.0 62.4 jit_solution(10798975578533101206)
XLA Ops:
  0.6 58.7 %shard_map.122 = (bf16[16,24,512]{2,1,0:T(8,128)(2,1)}, f32[8,128]{1,0:T(8,128)}) custom-call(bf16[16,512,256]{2,1,0:T(8,128)(2,1)} %bitcast.12, bf16[8,256,256]{2,1,0:T(8,128)(2,1)} %bitcast.13, bf16[4,128,256]{2,1,0:T(8,128)(2,1)} %bitcast.14, bf16[2,64,256]{2,1,0:T(8,128)(2,1)} %bitcast.15, s32[16,512]{1,0:T(8,128)} %bitcast.16, ...), custom_call_target="tpu_custom_call" | custom-call | tf_op jit(solution)/shard_map/pallas_call | solution.py:569
  59.3 1.2 %slice.7 = f32[1,1]{1,0:T(1,128)} slice(f32[8,128]{1,0:T(8,128)} %get-tuple-element.5), slice={[0:1], [0:1]} | slice | bytes 8 | tf_op jit(solution)/shard_map/slice | solution.py:585
  60.5 1.0 %slice_bitcast_fusion = bf16[1,19,16,512]{3,1,2,0:T(8,128)(2,1)S(1)} fusion(bf16[16,24,512]{2,1,0:T(8,128)(2,1)} %get-tuple-element.4), kind=kLoop, calls=%fused_computation | loop fusion | bytes 622592 | tf_op jit(solution)/shard_map/broadcast_in_dim | solution.py:585
  61.6 0.8 %copy.13 = bf16[1,19,16,512]{3,2,1,0:T(8,128)(2,1)} copy(bf16[1,19,16,512]{3,1,2,0:T(8,128)(2,1)S(1)} %slice_bitcast_fusion) | data formatting | bytes 622592

commit v2 on v1

v2 whole, which is shorter than its diff:
```python
import functools

import jax
import jax.numpy as jnp
from jax import lax
from jax.experimental import pallas as pl
from jax.experimental.pallas import tpu as pltpu
from jax.sharding import PartitionSpec as P

GROUPS = 32
NORM_FLOOR = 0.05
IGNORED = 255
Q_CHUNKS = 8
E_CHUNKS = 4
TICKS = (1, 2, 1, 2, 1, 1, 4)
MESH = pl.DeviceIdType.MESH
F32 = jnp.float32
BF16 = jnp.bfloat16


def phase(name):
    pass


def group_fold(x):
    width = x.shape[-1]
    lane = lax.broadcasted_iota(jnp.int32, x.shape, x.ndim - 1)
    step = 1
    while step < width // GROUPS:
        ahead = pltpu.roll(x, width - step, x.ndim - 1)
        behind = pltpu.roll(x, step, x.ndim - 1)
        x = x + jnp.where(lax.rem(lane, 2 * step) < step, ahead, behind)
        step *= 2
    return x


def doubling(rows, cols, source_axis):
    source = lax.broadcasted_iota(jnp.int32, (rows, cols), source_axis)
    target = lax.broadcasted_iota(jnp.int32, (rows, cols), 1 - source_axis)
    count = (rows, cols)[source_axis]
    near = lax.div(target, 2)
    far = jnp.clip(near + 2 * lax.rem(target, 2) - 1, 0, count - 1)
    return (
        0.75 * (source == near).astype(F32) + 0.25 * (source == far).astype(F32)
    ).astype(BF16)


def conv_block(x_ref, flat_ref, start, rows):
    cols, depth = x_ref.shape[1:]
    width = flat_ref.shape[1] // 3
    lhs = jnp.concatenate(
        [
            x_ref[pl.ds(start + down, rows)].reshape(rows * cols, depth)
            for down in range(3)
        ],
        axis=1,
    )
    taps = jnp.dot(lhs, flat_ref[...], preferred_element_type=F32)
    col = lax.rem(lax.broadcasted_iota(jnp.int32, (rows * cols, width), 0), cols)
    left = jnp.where(col == 0, 0.0, pltpu.roll(taps[:, :width], 1, 0))
    right = jnp.where(col == cols - 1, 0.0, pltpu.roll(taps[:, 2 * width :], rows * cols - 1, 0))
    return (taps[:, width : 2 * width] + left + right).reshape(rows, cols, width)


def conv_to(x_ref, flat_ref, y_ref, stat_ref, start, rows, offset):
    y = conv_block(x_ref, flat_ref, start, rows)
    cols = y.shape[1]
    y_ref[pl.ds(start + offset, rows)] = y
    sums = jnp.sum(y, axis=1, keepdims=True)
    centred = y - sums / cols
    stat_ref[pl.ds(start, rows), 0:1] = sums
    stat_ref[pl.ds(start, rows), 1:2] = jnp.sum(centred * centred, axis=1, keepdims=True)


def head_kernel(
    shape,
    q, e, s, t, labels_in, first_w, inner_w, gain_in, shift_in, class_w_in, bias_in,
    out, loss_out,
    labels, gain, shift, class_w, bias,
    q_in, e_in, s_in, t_in, w_q, w_e, w_s, w_t, w_i,
    q_y, e_y, s_y, t_y, s_grown, s_y2, t_grown, t_y2, t_grown2, t_y3,
    t_leave, s_leave, t_leave2, t_land, s_land, t_land2,
    q_stat, e_stat, s_stat, t_stat, s_stat2, t_stat2, t_stat3,
    slab, slabs, class_f, class_pad, up_t, up_s, coarse, wide, scores, loss_slab, loss_slabs,
    local_sem, edge_send, edge_recv, slab_send, slab_recv, loss_send, loss_recv,
):
    size, images = shape["rows"], shape["batch"]
    total = size * images
    me, image = lax.axis_index("rows"), lax.axis_index("batch")
    flat = image * size + me
    width = q_y.shape[2]
    classes = class_w.shape[0]

    def device_at(distance):
        number = lax.rem(flat + distance, total)
        return {"batch": lax.div(number, size), "rows": lax.rem(number, size)}

    phase("enter")
    barrier = pltpu.get_barrier_semaphore()

    def greet(distance, carry):
        pl.semaphore_signal(
            barrier, inc=1, device_id=device_at(distance), device_id_type=MESH
        )
        return carry

    lax.fori_loop(1, total, greet, 0)

    fetched = []

    def fetch(source, target):
        copy = pltpu.make_async_copy(source, target, local_sem.at[len(fetched)])
        copy.start()
        fetched.append(copy)
        return copy

    def fetch_weights(source, target):
        depth = source.shape[2]
        done = local_sem.at[len(fetched)]
        for down in range(3):
            for across in range(3):
                place = target.at[
                    down * depth : (down + 1) * depth, across * width : (across + 1) * width
                ]
                pltpu.make_async_copy(source.at[down, across], place, done).start()
        fetched.append(pltpu.make_async_copy(target, target, done))
        return [fetched[-1]]

    def settle(copies):
        for copy in copies:
            copy.wait()

    q_rows, q_cols = q.shape[:2]
    e_rows, s_rows, t_rows = e.shape[0], s.shape[0], t.shape[0]
    e_cols, s_cols, t_cols = e.shape[1], s.shape[1], t.shape[1]
    got_t = [fetch(t, t_in.at[1 : t_rows + 1])]
    got_s = [fetch(s, s_in.at[1 : s_rows + 1])]
    got_q = fetch_weights(first_w.at[0], w_q) + [fetch(q, q_in.at[1 : q_rows + 1])]
    got_w_t = fetch_weights(first_w.at[3], w_t)
    got_w_s = fetch_weights(first_w.at[2], w_s)
    got_small = [
        fetch(class_w_in, class_w),
        fetch(bias_in, bias),
        fetch(gain_in, gain),
        fetch(shift_in, shift),
        fetch(labels_in, labels),
    ]
    got_i = [fetch_weights(inner_w.at[i], w_i.at[i]) for i in range(3)]
    got_e = fetch_weights(first_w.at[1], w_e) + [fetch(e, e_in.at[1 : e_rows + 1])]

    def exists(offset):
        return me + offset < size if offset > 0 else me + offset >= 0

    def neighbour(offset):
        return {"rows": lax.rem(me + offset + size, size)}

    def edges(lower, upper, before, after, number):
        return [
            (
                pltpu.make_async_remote_copy(
                    src_ref=source,
                    dst_ref=target,
                    send_sem=edge_send.at[number + place],
                    recv_sem=edge_recv.at[number + place],
                    device_id=neighbour(offset),
                    device_id_type=MESH,
                ),
                offset,
            )
            for place, (source, target, offset) in enumerate([(lower, before, 1), (upper, after, -1)])
        ]

    def send(pairs):
        for copy, offset in pairs:
            pl.when(exists(offset))(copy.start)

    def arrive(pairs):
        for copy, offset in pairs:
            pl.when(exists(-offset))(copy.wait_recv)

    def leave(pairs):
        for copy, offset in pairs:
            pl.when(exists(offset))(copy.wait_send)

    def band_edges(field, number):
        last = field.shape[0] - 1
        return edges(field.at[last - 1], field.at[1], field.at[0], field.at[last], number)

    def line_edges(leaving, landing, number):
        return edges(leaving.at[1], leaving.at[0], landing.at[0], landing.at[1], number)

    t_edges, s_edges = band_edges(t_in, 0), band_edges(s_in, 2)
    t_y_edges, s_y_edges = line_edges(t_leave, t_land, 4), line_edges(s_leave, s_land, 6)
    t_y2_edges, coarse_edges = line_edges(t_leave2, t_land2, 8), band_edges(coarse, 10)

    def chunk_edges(source, framed, number, part=slice(None)):
        last = source.shape[0] - 1
        return edges(
            source.at[last, part],
            source.at[0, part],
            framed.at[0, part],
            framed.at[last + 2, part],
            number,
        )

    def parts(cols, count):
        return [pl.ds(k * (cols // count), cols // count) for k in range(count)]

    e_edges, q_edges = chunk_edges(e, e_in, 12), chunk_edges(q, q_in, 14)
    chunks = [chunk_edges(e, e_in, 12, part) for part in parts(e_cols, E_CHUNKS)]
    chunks += [chunk_edges(q, q_in, 14, part) for part in parts(q_cols, Q_CHUNKS)]
    waiting, ticks = list(chunks), list(TICKS)

    def tick():
        for _ in range(ticks.pop(0)):
            send(waiting.pop(0))

    @pl.when(me == 0)
    def _():
        for field in (q_in, e_in, s_in, t_in):
            field[0] = jnp.zeros(field.shape[1:], BF16)

    @pl.when(me == size - 1)
    def _():
        for field in (q_in, e_in, s_in, t_in):
            field[field.shape[0] - 1] = jnp.zeros(field.shape[1:], BF16)

    up_t[...] = doubling(*up_t.shape, 1)
    up_s[...] = doubling(*up_s.shape, 1)

    phase("barrier")
    pl.semaphore_wait(barrier, total - 1)
    phase("send_ts")
    settle(got_t)
    send(t_edges)
    settle(got_s)
    send(s_edges)

    def slab_copy(number, distance, sender):
        return pltpu.make_async_remote_copy(
            src_ref=slab.at[number],
            dst_ref=slabs.at[number, sender],
            send_sem=slab_send.at[number],
            recv_sem=slab_recv.at[number],
            device_id=neighbour(distance),
            device_id_type=MESH,
        )

    def slab_all(number):
        rest = slabs.at[number, 0 : size - 1]
        return pltpu.make_async_remote_copy(
            src_ref=rest,
            dst_ref=rest,
            send_sem=slab_send.at[number],
            recv_sem=slab_recv.at[number],
            device_id=neighbour(1),
            device_id_type=MESH,
        )

    def announce(number, stat, cols):
        rows = stat.shape[0]
        sums = stat[:, 0:1]
        channel = jnp.sum(sums, axis=0)
        mean = group_fold(channel) / (rows * cols * (width // GROUPS))
        strays = sums / cols - mean
        slab[number, 0:1] = channel
        slab[number, 1:2] = jnp.sum(stat[:, 1:2] + cols * (strays * strays), axis=0)
        for distance in range(1, size):
            slab_copy(number, distance, me).start()
        slabs[number, me] = slab[number]

    def gather(number, rows, cols):
        slab_all(number).wait_recv()
        count = rows * cols * (width // GROUPS)
        every = slabs[number].reshape(2 * size, width)
        every = group_fold(every).reshape(size, 2, width)
        means = every[:, 0:1] / count
        mean = jnp.sum(means, axis=0) / size
        strays = means - mean
        squares = jnp.sum(every[:, 1:2] + count * (strays * strays), axis=0)
        return mean, squares / (count * size)

    def activation(stat, layer):
        mean, var = stat
        factor = gain[layer : layer + 1] * lax.rsqrt(var + NORM_FLOOR)
        offset = shift[layer : layer + 1]
        return lambda y: jnp.maximum((y - mean) * factor + offset, 0.0).astype(BF16)

    def part_with(field, leaving, number, pairs):
        own = field.shape[0] - 2
        mean = slab[number, 0:1] / (own * field.shape[1])
        leaving[0] = (field[1] - mean).astype(BF16)
        leaving[1] = (field[own] - mean).astype(BF16)
        send(pairs)

    def frame(field, landing, number, pairs):
        own = field.shape[0] - 2
        arrive(pairs)

        def accept(place, row, sender):
            mean = slabs[number, sender, 0:1] / (own * field.shape[1])
            field[row] = landing[place].astype(F32) + mean

        pl.when(me > 0)(lambda: accept(0, 0, lax.rem(me - 1 + size, size)))
        pl.when(me < size - 1)(lambda: accept(1, own + 1, lax.rem(me + 1, size)))

        @pl.when(me == 0)
        def _():
            field[0] = field[1]

        @pl.when(me == size - 1)
        def _():
            field[own + 1] = field[own]

    def grow(field, grown, up, act):
        own = field.shape[0] - 2
        lines = jnp.concatenate([act(field[row]) for row in range(own + 2)], axis=1)
        lines = jnp.dot(up[...], lines, preferred_element_type=F32)
        for row in range(own + 1):
            here = lines[:, row * width : (row + 1) * width]
            below = lines[:, (row + 1) * width : (row + 2) * width]
            grown[2 * row] = (0.75 * here + 0.25 * below).astype(BF16)
            grown[2 * row + 1] = (0.25 * here + 0.75 * below).astype(BF16)

        @pl.when(me == 0)
        def _():
            grown[0] = jnp.zeros(grown.shape[1:], BF16)

        @pl.when(me == size - 1)
        def _():
            grown[2 * own + 1] = jnp.zeros(grown.shape[1:], BF16)

    def convolve(x_ref, flat_ref, y_ref, stat_ref, offset):
        count, cols = x_ref.shape[0] - 2, x_ref.shape[1]
        rows = max(r for r in range(1, count + 1) if count % r == 0 and (r == 1 or r * cols <= 1024))

        def step(index, carry):
            conv_to(x_ref, flat_ref, y_ref, stat_ref, index * rows, rows, offset)
            return carry

        lax.fori_loop(0, count // rows, step, 0)

    def q_blocks(first, last):
        def step(index, carry):
            conv_to(q_in, w_q, q_y, q_stat, 1 + 2 * index, 2, 0)
            return carry

        lax.fori_loop(first, last, step, 0)

    blocks = (q_rows - 2) // 2
    phase("fetch_q")
    settle(got_q)
    phase("q_blocks_a")
    q_blocks(0, 2)
    tick()
    phase("wait_t")
    settle(got_w_t)
    arrive(t_edges)
    phase("conv_t")
    conv_to(t_in, w_t, t_y, t_stat, 0, t_rows, 1)
    phase("announce_t")
    announce(0, t_stat, t_cols)
    part_with(t_y, t_leave, 0, t_y_edges)
    phase("wait_s")
    settle(got_w_s)
    arrive(s_edges)
    phase("conv_s")
    conv_to(s_in, w_s, s_y, s_stat, 0, s_rows, 1)
    announce(1, s_stat, s_cols)
    part_with(s_y, s_leave, 1, s_y_edges)
    tick()
    phase("q_blocks_b")
    settle(got_small)
    q_blocks(2, 3)
    phase("gather_t")
    norm = gather(0, t_rows, t_cols)
    settle(got_i[1])
    phase("frame_t")
    frame(t_y, t_land, 0, t_y_edges)
    phase("grow_t")
    grow(t_y, t_grown, up_t, activation(norm, 3))
    phase("conv_t2")
    convolve(t_grown, w_i.at[1], t_y2, t_stat2, 1)
    phase("announce_t2")
    announce(2, t_stat2, 2 * t_cols)
    part_with(t_y2, t_leave2, 2, t_y2_edges)
    tick()
    phase("gather_s")
    norm = gather(1, s_rows, s_cols)
    settle(got_i[0])
    phase("frame_s")
    frame(s_y, s_land, 1, s_y_edges)
    phase("grow_s")
    grow(s_y, s_grown, up_s, activation(norm, 2))
    phase("conv_s2")
    convolve(s_grown, w_i.at[0], s_y2, s_stat2, 0)
    announce(3, s_stat2, 2 * s_cols)
    tick()
    phase("q_blocks_c")
    q_blocks(3, 4)
    phase("gather_t2")
    norm = gather(2, 2 * t_rows, 2 * t_cols)
    settle(got_i[2])
    tick()
    phase("frame_t2")
    frame(t_y2, t_land2, 2, t_y2_edges)
    phase("grow_t2")
    grow(t_y2, t_grown2, up_s, activation(norm, 5))
    phase("conv_t3")
    convolve(t_grown2, w_i.at[2], t_y3, t_stat3, 0)
    phase("announce_t3")
    announce(4, t_stat3, 4 * t_cols)
    tick()
    phase("wait_e")
    settle(got_e)
    arrive(e_edges)
    phase("conv_e")
    convolve(e_in, w_e, e_y, e_stat, 0)
    announce(5, e_stat, e_cols)
    tick()
    phase("q_blocks_d")
    q_blocks(4, blocks)
    phase("wait_q")
    arrive(q_edges)
    phase("conv_q_border")

    def border(index, carry):
        conv_to(q_in, w_q, q_y, q_stat, index * (q_rows - 1), 1, 0)
        return carry

    lax.fori_loop(0, 2, border, 0)
    announce(6, q_stat, q_cols)

    phase("gather_t3")
    t_act = activation(gather(4, 4 * t_rows, 4 * t_cols), 6)
    phase("gather_se")
    s_act = activation(gather(3, 2 * s_rows, 2 * s_cols), 4)
    e_act = activation(gather(5, e_rows, e_cols), 1)
    phase("project")
    class_f[...] = jnp.zeros(class_f.shape, F32)
    class_f[0:classes] = class_w[...].astype(F32)
    class_pad[...] = class_f[...].astype(BF16)
    padded = class_f.shape[0]
    weight = class_pad[...]
    weights = jnp.concatenate([weight] * 3, axis=1)
    across = (((1,), (1,)), ((), ()))

    def project(row, carry):
        lines = jnp.concatenate([e_act(e_y[row]), s_act(s_y2[row]), t_act(t_y3[row])], axis=1)
        coarse[row + 1] = lax.dot_general(weights, lines, across, preferred_element_type=F32)
        return carry

    lax.fori_loop(0, e_rows, project, 0, unroll=2)
    send(coarse_edges)

    phase("gather_q")
    q_act = activation(gather(6, q_rows, q_cols), 0)
    spot = lax.broadcasted_iota(jnp.int32, (padded, classes), 0)
    lane = lax.broadcasted_iota(jnp.int32, (padded, classes), 1)
    bias_col = jnp.sum(jnp.where(spot == lane, bias[...], 0.0), axis=1, keepdims=True)
    phase("score_q")

    def score(row, carry):
        scores[row] = (
            lax.dot_general(weight, q_act(q_y[row]), across, preferred_element_type=F32) + bias_col
        )
        return carry

    lax.fori_loop(0, q_rows, score, 0, unroll=4)
    phase("wait_coarse")
    up_cols = doubling(e_cols, q_cols, 0)
    arrive(coarse_edges)

    @pl.when(me == 0)
    def _():
        coarse[0] = coarse[1]

    @pl.when(me == size - 1)
    def _():
        coarse[e_rows + 1] = coarse[e_rows]

    phase("widen")
    lines = coarse[...].reshape((e_rows + 2) * padded, e_cols)
    high = lines.astype(BF16)
    low = (lines - high.astype(F32)).astype(BF16)
    lines = jnp.dot(high, up_cols, preferred_element_type=F32) + jnp.dot(
        low, up_cols, preferred_element_type=F32
    )
    wide[...] = lines.reshape(wide.shape)
    phase("finish")
    kind = lax.broadcasted_iota(jnp.int32, (padded, q_cols), 0)

    def finish(row, grown):
        line = scores[row] + grown
        scores[row] = line
        powers = jnp.where(kind < classes, jnp.exp(line), 0.0)
        log_total = jnp.log(jnp.sum(powers, axis=0, keepdims=True))
        label = labels[pl.ds(row, 1), :]
        picked = jnp.sum(jnp.where(kind == label, line, 0.0), axis=0, keepdims=True)
        usable = label != IGNORED
        return jnp.where(usable, log_total - picked, 0.0), usable.astype(F32)

    def pair(index, carry):
        here = wide[index + 1]
        upper = finish(2 * index, 0.25 * wide[index] + 0.75 * here)
        lower = finish(2 * index + 1, 0.75 * here + 0.25 * wide[index + 2])
        return carry[0] + upper[0] + lower[0], carry[1] + upper[1] + lower[1]

    zero = jnp.zeros((1, q_cols), F32)
    sums = lax.fori_loop(0, e_rows, pair, (zero, zero), unroll=2)
    phase("loss_send")
    for place, line in enumerate(sums):
        loss_slab[place : place + 1] = sum(
            line[:, k * width : (k + 1) * width] for k in range(q_cols // width)
        )

    def loss_copy(source, target, distance):
        return pltpu.make_async_remote_copy(
            src_ref=source,
            dst_ref=target,
            send_sem=loss_send.at[0],
            recv_sem=loss_recv.at[0],
            device_id=device_at(distance),
            device_id_type=MESH,
        )

    def loss_go(distance, carry):
        loss_copy(loss_slab, loss_slabs.at[flat], distance).start()
        return carry

    rest = loss_slabs.at[0 : total - 1]
    loss_all = loss_copy(rest, rest, 1)

    lax.fori_loop(1, total, loss_go, 0)
    loss_slabs[flat] = loss_slab[...]
    phase("output")
    for first in range(0, classes, 8):
        lines = jnp.transpose(scores[:, first : first + 8], (1, 0, 2)).astype(BF16)
        out[first : min(first + 8, classes)] = lines[: min(8, classes - first)]
    phase("leave")
    for pairs in (
        t_edges, s_edges, t_y_edges, s_y_edges, t_y2_edges, coarse_edges, e_edges, q_edges,
    ):
        leave(pairs)
    for number in range(slab.shape[0]):
        slab_all(number).wait_send()
    phase("loss_wait")
    loss_all.wait_recv()
    phase("loss_end")
    ends = jnp.sum(jnp.sum(loss_slabs[...], axis=0), axis=1, keepdims=True)
    loss_out[...] = jnp.broadcast_to(ends[0:1] / jnp.maximum(ends[1:2], 1.0), loss_out.shape)
    loss_all.wait_send()
    phase("")


def make_per_device(shape):
    def per_device(
        feat_quarter,
        feat_eighth,
        feat_sixteenth,
        feat_thirty,
        labels,
        first_weights,
        inner_weights,
        norm_gain,
        norm_shift,
        class_weight,
        class_bias,
    ):
        q, e, s, t = feat_quarter[0], feat_eighth[0], feat_sixteenth[0], feat_thirty[0]
        size = shape["rows"]
        total = size * shape["batch"]
        depth, width = first_weights.shape[3:]
        classes = class_weight.shape[1]
        padded = -(-classes // 8) * 8
        (q_rows, q_cols), (e_rows, e_cols) = q.shape[:2], e.shape[:2]
        (s_rows, s_cols), (t_rows, t_cols) = s.shape[:2], t.shape[:2]

        def framed(rows, cols, channels, kind=BF16):
            return pltpu.VMEM((rows + 2, cols, channels), kind)

        def field(rows, cols):
            return pltpu.VMEM((rows, cols, width), F32)

        def stat(rows):
            return pltpu.VMEM((rows, 8, width), F32)

        def line(cols):
            return pltpu.VMEM((2, cols, width), BF16)

        small = [labels[0], norm_gain, norm_shift, class_weight.T, class_bias[None]]
        scratch = [
            *[pltpu.VMEM(x.shape, x.dtype) for x in small],
            framed(q_rows, q_cols, depth),
            framed(e_rows, e_cols, depth),
            framed(s_rows, s_cols, depth),
            framed(t_rows, t_cols, depth),
            *[pltpu.VMEM((3 * depth, 3 * width), BF16)] * 4,
            pltpu.VMEM((3, 3 * width, 3 * width), BF16),
            field(q_rows, q_cols),
            field(e_rows, e_cols),
            framed(s_rows, s_cols, width, F32),
            framed(t_rows, t_cols, width, F32),
            framed(2 * s_rows, 2 * s_cols, width),
            field(2 * s_rows, 2 * s_cols),
            framed(2 * t_rows, 2 * t_cols, width),
            framed(2 * t_rows, 2 * t_cols, width, F32),
            framed(4 * t_rows, 4 * t_cols, width),
            field(4 * t_rows, 4 * t_cols),
            *[line(cols) for cols in (t_cols, s_cols, 2 * t_cols)] * 2,
            stat(q_rows),
            stat(e_rows),
            stat(s_rows),
            stat(t_rows),
            stat(2 * s_rows),
            stat(2 * t_rows),
            stat(4 * t_rows),
            pltpu.VMEM((7, 2, width), F32),
            pltpu.VMEM((7, size, 2, width), F32),
            pltpu.VMEM((padded, width), F32),
            pltpu.VMEM((padded, width), BF16),
            pltpu.VMEM((2 * t_cols, t_cols), BF16),
            pltpu.VMEM((2 * s_cols, s_cols), BF16),
            framed(e_rows, padded, e_cols, F32),
            framed(e_rows, padded, q_cols, F32),
            pltpu.VMEM((q_rows, padded, q_cols), F32),
            pltpu.VMEM((2, width), F32),
            pltpu.VMEM((total, 2, width), F32),
            *[pltpu.SemaphoreType.DMA((count,)) for count in (17, 16, 16, 7, 7, 1, 1)],
        ]
        away, held = pl.BlockSpec(memory_space=pl.ANY), pl.BlockSpec(memory_space=pltpu.VMEM)
        operands = (q, e, s, t, small[0], first_weights, inner_weights, *small[1:])
        logits, loss = pl.pallas_call(
            functools.partial(head_kernel, shape),
            out_shape=(
                jax.ShapeDtypeStruct((classes, q_rows, q_cols), BF16),
                jax.ShapeDtypeStruct((8, width), F32),
            ),
            in_specs=[away] * 11,
            out_specs=(held, held),
            scratch_shapes=scratch,
            compiler_params=pltpu.CompilerParams(
                collective_id=0, has_side_effects=True, vmem_limit_bytes=32 << 20
            ),
        )(*[pltpu.with_memory_space_constraint(x, pltpu.HBM) for x in operands])
        return (logits[None], loss[0, 0])

    return per_device


def solution(mesh):
    in_specs = (
        P("batch", "rows", None, None),
        P("batch", "rows", None, None),
        P("batch", "rows", None, None),
        P("batch", "rows", None, None),
        P("batch", "rows", None),
        P(),
        P(),
        P(),
        P(),
        P(),
        P(),
    )
    out_specs = (P("batch", None, "rows", None), P())
    return jax.shard_map(
        make_per_device(dict(mesh.shape)),
        mesh=mesh,
        in_specs=in_specs,
        out_specs=out_specs,
        check_vma=False,
    )
```

time: 62.6 us -> 50.3 us (0.80)
  Pallas kernels: 58.7 us -> 48.2 us
  local copies, waits for them, and re-layouts: 3.02 us -> 1.23 us
    pallas_call x1, Pallas kernels: 58.7 us -> 48.2 us  [per_device(): pl.pallas_call(functools.partial(head_kernel, shape), out_shape=(jax.Shap...]
    broadcast_in_dim x1 -> x0, local copies, waits for them, and re-layouts: 1.02 us -> none  [per_device(): return (scores[:, :classes].transpose(1, 0, 2)[None], loss[0, 0])]
    slice x1, local copies, waits for them, and re-layouts: 1.18 us -> 0.51 us  [per_device(): return (logits[None], loss[0, 0])]
where the time goes in v2:
time: 50.3 us; the launch traced here: 50.1 us
  Pallas kernels  48.2 us (96%)
  local copies, waits for them, and re-layouts  1.23 us (2%)
  between operations  0.64 us (1%)
    pallas_call x1, Pallas kernels, per_device(): pl.pallas_call(functools.partial(head_kernel, shape), out_shape=(jax.Shap...  48.2 us

profile of v2, /device:TPU:0, one launch (start us, length us, event | category | flops | bytes accessed | tf_op | source)
XLA Modules:
  0.0 50.1 jit_solution(3116354582998837585)
XLA Ops:
  0.6 48.2 %shard_map.122 = (bf16[19,16,512]{2,1,0:T(8,128)(2,1)S(1)}, f32[8,128]{1,0:T(8,128)S(1)}) custom-call(bf16[16,512,256]{2,1,0:T(8,128)(2,1)} %bitcast.10, bf16[8,256,256]{2,1,0:T(8,128)(2,1)} %bitcast.11, bf16[4,128,256]{2,1,0:T(8,128)(2,1)} %bitcast.12, bf16[2,64,256]{2,1,0:T(8,128)(2,1)} %bitcast.13, s32[16,512]{1,0:T(8,128)} %bitcast.14, ...), custom_call_target="tpu_custom_call" | custom-call | tf_op jit(solution)/shard_map/pallas_call | solution.py:633
  48.9 0.5 %slice.3 = f32[1,1]{1,0:T(1,128)} slice(f32[8,128]{1,0:T(8,128)S(1)} %get-tuple-element.5), slice={[0:1], [0:1]} | slice | bytes 8 | tf_op jit(solution)/shard_map/slice | solution.py:646
  49.4 0.7 %copy.14 = bf16[1,19,16,512]{3,2,1,0:T(8,128)(2,1)} copy(bf16[1,19,16,512]{3,2,1,0:T(8,128)(2,1)S(1)} %bitcast.9) | data formatting | bytes 622592

commit v3 on v2

--- a/solution.py
+++ b/solution.py
@@ -10,9 +10,10 @@
 GROUPS = 32
 NORM_FLOOR = 0.05
 IGNORED = 255
-Q_CHUNKS = 8
-E_CHUNKS = 4
-TICKS = (1, 2, 1, 2, 1, 1, 4)
+Q_CHUNKS = 4
+E_CHUNKS = 2
+TICKS = (1, 1, 1, 1, 1, 1)
+PAIRS = (3, 2, 1, 2)
 MESH = pl.DeviceIdType.MESH
 F32 = jnp.float32
 BF16 = jnp.bfloat16
@@ -45,31 +46,33 @@
     ).astype(BF16)
 
 
-def conv_block(x_ref, flat_ref, start, rows):
-    cols, depth = x_ref.shape[1:]
-    width = flat_ref.shape[1] // 3
-    lhs = jnp.concatenate(
-        [
-            x_ref[pl.ds(start + down, rows)].reshape(rows * cols, depth)
-            for down in range(3)
-        ],
-        axis=1,
-    )
-    taps = jnp.dot(lhs, flat_ref[...], preferred_element_type=F32)
-    col = lax.rem(lax.broadcasted_iota(jnp.int32, (rows * cols, width), 0), cols)
+def conv_block(lines, flat, rows):
+    width = flat.shape[1] // 3
+    count = lines.shape[0]
+    cols = count // rows
+    taps = jnp.dot(lines, flat, preferred_element_type=F32)
+    col = lax.rem(lax.broadcasted_iota(jnp.int32, (count, width), 0), cols)
     left = jnp.where(col == 0, 0.0, pltpu.roll(taps[:, :width], 1, 0))
-    right = jnp.where(col == cols - 1, 0.0, pltpu.roll(taps[:, 2 * width :], rows * cols - 1, 0))
+    right = jnp.where(col == cols - 1, 0.0, pltpu.roll(taps[:, 2 * width :], count - 1, 0))
     return (taps[:, width : 2 * width] + left + right).reshape(rows, cols, width)
 
 
-def conv_to(x_ref, flat_ref, y_ref, stat_ref, start, rows, offset):
-    y = conv_block(x_ref, flat_ref, start, rows)
-    cols = y.shape[1]
+def keep(y, y_ref, stat_ref, start, offset):
+    rows, cols = y.shape[:2]
     y_ref[pl.ds(start + offset, rows)] = y
     sums = jnp.sum(y, axis=1, keepdims=True)
     centred = y - sums / cols
     stat_ref[pl.ds(start, rows), 0:1] = sums
     stat_ref[pl.ds(start, rows), 1:2] = jnp.sum(centred * centred, axis=1, keepdims=True)
+
+
+def conv_to(x_ref, flat_ref, y_ref, stat_ref, start, rows, offset):
+    cols, depth = x_ref.shape[1:]
+    lines = [
+        x_ref[pl.ds(start + down, rows)].reshape(rows * cols, depth) for down in range(3)
+    ]
+    y = conv_block(jnp.concatenate(lines, axis=1), flat_ref[...], rows)
+    keep(y, y_ref, stat_ref, start, offset)
 
 
 def head_kernel(
@@ -79,7 +82,8 @@
     labels, gain, shift, class_w, bias,
     q_in, e_in, s_in, t_in, w_q, w_e, w_s, w_t, w_i,
     q_y, e_y, s_y, t_y, s_grown, s_y2, t_grown, t_y2, t_grown2, t_y3,
-    t_leave, s_leave, t_leave2, t_land, s_land, t_land2,
+    t_leave, s_leave, t_leave2, e_leave, q_leave, t_land, s_land, t_land2, e_land, q_land,
+    base_leave, base_land,
     q_stat, e_stat, s_stat, t_stat, s_stat2, t_stat2, t_stat3,
     slab, slabs, class_f, class_pad, up_t, up_s, coarse, wide, scores, loss_slab, loss_slabs,
     local_sem, edge_send, edge_recv, slab_send, slab_recv, loss_send, loss_recv,
@@ -193,22 +197,18 @@
     t_y_edges, s_y_edges = line_edges(t_leave, t_land, 4), line_edges(s_leave, s_land, 6)
     t_y2_edges, coarse_edges = line_edges(t_leave2, t_land2, 8), band_edges(coarse, 10)
 
-    def chunk_edges(source, framed, number, part=slice(None)):
-        last = source.shape[0] - 1
-        return edges(
-            source.at[last, part],
-            source.at[0, part],
-            framed.at[0, part],
-            framed.at[last + 2, part],
-            number,
-        )
-
-    def parts(cols, count):
-        return [pl.ds(k * (cols // count), cols // count) for k in range(count)]
-
-    e_edges, q_edges = chunk_edges(e, e_in, 12), chunk_edges(q, q_in, 14)
-    chunks = [chunk_edges(e, e_in, 12, part) for part in parts(e_cols, E_CHUNKS)]
-    chunks += [chunk_edges(q, q_in, 14, part) for part in parts(q_cols, Q_CHUNKS)]
+    def part_edges(leaving, landing, number, chunks):
+        step = leaving.shape[1] // chunks
+        return [
+            edges(
+                leaving.at[1, part], leaving.at[0, part], landing.at[0, part], landing.at[1, part], number
+            )
+            for part in (pl.ds(k * step, step) for k in range(chunks))
+        ]
+
+    e_edges, q_edges = line_edges(e_leave, e_land, 12), line_edges(q_leave, q_land, 14)
+    base_edges = line_edges(base_leave, base_land, 16)
+    chunks = part_edges(e_leave, e_land, 12, E_CHUNKS) + part_edges(q_leave, q_land, 14, Q_CHUNKS)
     waiting, ticks = list(chunks), list(TICKS)
 
     def tick():
@@ -217,13 +217,17 @@
 
     @pl.when(me == 0)
     def _():
-        for field in (q_in, e_in, s_in, t_in):
+        for field in (s_in, t_in):
             field[0] = jnp.zeros(field.shape[1:], BF16)
 
     @pl.when(me == size - 1)
     def _():
-        for field in (q_in, e_in, s_in, t_in):
+        for field in (s_in, t_in):
             field[field.shape[0] - 1] = jnp.zeros(field.shape[1:], BF16)
+
+    for field in (q_in, e_in):
+        for row in (0, field.shape[0] - 1):
+            field[row] = jnp.zeros(field.shape[1:], BF16)
 
     up_t[...] = doubling(*up_t.shape, 1)
     up_s[...] = doubling(*up_s.shape, 1)
@@ -233,8 +237,6 @@
     phase("send_ts")
     settle(got_t)
     send(t_edges)
-    settle(got_s)
-    send(s_edges)
 
     def slab_copy(number, distance, sender):
         return pltpu.make_async_remote_copy(
@@ -340,18 +342,49 @@
 
         lax.fori_loop(0, count // rows, step, 0)
 
-    def q_blocks(first, last):
+    done, pairs_left = [0], list(PAIRS)
+
+    def q_blocks():
+        first, last = done[0], done[0] + pairs_left.pop(0)
+        done[0] = last = last if pairs_left else q_rows // 2
+
         def step(index, carry):
-            conv_to(q_in, w_q, q_y, q_stat, 1 + 2 * index, 2, 0)
+            conv_to(q_in, w_q, q_y, q_stat, 2 * index, 2, 0)
             return carry
 
         lax.fori_loop(first, last, step, 0)
 
-    blocks = (q_rows - 2) // 2
+    def lend(x_ref, flat_ref, leaving, place):
+        depth, last = x_ref.shape[2], x_ref.shape[0] - 2
+        for side, row, down in ((0, 1, 2), (1, last, 0)):
+            flat = flat_ref[down * depth : (down + 1) * depth]
+            term = conv_block(x_ref[row], flat, 1)[0]
+            base = jnp.sum(term, axis=0, keepdims=True) / term.shape[0]
+            leaving[side] = (term - base).astype(BF16)
+            base_leave[side, place : place + 1] = base
+
+    def mend(y_ref, stat_ref, landing, place, pairs):
+        arrive(pairs)
+
+        def add(side, row):
+            term = landing[side].astype(F32) + base_land[side, place : place + 1]
+            keep((y_ref[row] + term)[None], y_ref, stat_ref, row, 0)
+
+        pl.when(me > 0)(lambda: add(0, 0))
+        pl.when(me < size - 1)(lambda: add(1, y_ref.shape[0] - 1))
+
     phase("fetch_q")
     settle(got_q)
+    phase("lend_q")
+    lend(q_in, w_q, q_leave, 0)
+    settle(got_s)
+    send(s_edges)
     phase("q_blocks_a")
-    q_blocks(0, 2)
+    q_blocks()
+    phase("lend_e")
+    settle(got_e)
+    lend(e_in, w_e, e_leave, 1)
+    send(base_edges)
     tick()
     phase("wait_t")
     settle(got_w_t)
@@ -371,7 +404,7 @@
     tick()
     phase("q_blocks_b")
     settle(got_small)
-    q_blocks(2, 3)
+    q_blocks()
     phase("gather_t")
     norm = gather(0, t_rows, t_cols)
     settle(got_i[1])
@@ -397,7 +430,7 @@
     announce(3, s_stat2, 2 * s_cols)
     tick()
     phase("q_blocks_c")
-    q_blocks(3, 4)
+    q_blocks()
     phase("gather_t2")
     norm = gather(2, 2 * t_rows, 2 * t_cols)
     settle(got_i[2])
@@ -412,23 +445,15 @@
     announce(4, t_stat3, 4 * t_cols)
     tick()
     phase("wait_e")
-    settle(got_e)
-    arrive(e_edges)
-    phase("conv_e")
     convolve(e_in, w_e, e_y, e_stat, 0)
+    arrive(base_edges)
+    phase("mend_e")
+    mend(e_y, e_stat, e_land, 1, e_edges)
     announce(5, e_stat, e_cols)
-    tick()
     phase("q_blocks_d")
-    q_blocks(4, blocks)
-    phase("wait_q")
-    arrive(q_edges)
-    phase("conv_q_border")
-
-    def border(index, carry):
-        conv_to(q_in, w_q, q_y, q_stat, index * (q_rows - 1), 1, 0)
-        return carry
-
-    lax.fori_loop(0, 2, border, 0)
+    q_blocks()
+    phase("mend_q")
+    mend(q_y, q_stat, q_land, 0, q_edges)
     announce(6, q_stat, q_cols)
 
     phase("gather_t3")
@@ -539,7 +564,7 @@
         out[first : min(first + 8, classes)] = lines[: min(8, classes - first)]
     phase("leave")
     for pairs in (
-        t_edges, s_edges, t_y_edges, s_y_edges, t_y2_edges, coarse_edges, e_edges, q_edges,
+        t_edges, s_edges, t_y_edges, s_y_edges, t_y2_edges, coarse_edges, e_edges, q_edges, base_edges,
     ):
         leave(pairs)
     for number in range(slab.shape[0]):
@@ -607,7 +632,8 @@
             framed(2 * t_rows, 2 * t_cols, width, F32),
             framed(4 * t_rows, 4 * t_cols, width),
             field(4 * t_rows, 4 * t_cols),
-            *[line(cols) for cols in (t_cols, s_cols, 2 * t_cols)] * 2,
+            *[line(cols) for cols in (t_cols, s_cols, 2 * t_cols, e_cols, q_cols)] * 2,
+            *[pltpu.VMEM((2, 2, width), F32)] * 2,
             stat(q_rows),
             stat(e_rows),
             stat(s_rows),
@@ -626,7 +652,7 @@
             pltpu.VMEM((q_rows, padded, q_cols), F32),
             pltpu.VMEM((2, width), F32),
             pltpu.VMEM((total, 2, width), F32),
-            *[pltpu.SemaphoreType.DMA((count,)) for count in (17, 16, 16, 7, 7, 1, 1)],
+            *[pltpu.SemaphoreType.DMA((count,)) for count in (17, 18, 18, 7, 7, 1, 1)],
         ]
         away, held = pl.BlockSpec(memory_space=pl.ANY), pl.BlockSpec(memory_space=pltpu.VMEM)
         operands = (q, e, s, t, small[0], first_weights, inner_weights, *small[1:])

time: 50.3 us -> 42.5 us (0.84)
  Pallas kernels: 48.2 us -> 40.5 us
    pallas_call x1, Pallas kernels: 48.2 us -> 40.5 us  [per_device(): pl.pallas_call(functools.partial(head_kernel, shape), out_shape=(jax.Shap...]
where the time goes in v3:
time: 42.5 us; the launch traced here: 42.4 us
  Pallas kernels  40.5 us (95%)
  local copies, waits for them, and re-layouts  1.23 us (3%)
  between operations  0.64 us (2%)
    pallas_call x1, Pallas kernels, per_device(): pl.pallas_call(functools.partial(head_kernel, shape), out_shape=(jax.Shap...  40.5 us

profile of v3, /device:TPU:0, one launch (start us, length us, event | category | flops | bytes accessed | tf_op | source)
XLA Modules:
  0.0 42.4 jit_solution(4996199690183681484)
XLA Ops:
  0.6 40.5 %shard_map.122 = (bf16[19,16,512]{2,1,0:T(8,128)(2,1)S(1)}, f32[8,128]{1,0:T(8,128)S(1)}) custom-call(bf16[16,512,256]{2,1,0:T(8,128)(2,1)} %bitcast.10, bf16[8,256,256]{2,1,0:T(8,128)(2,1)} %bitcast.11, bf16[4,128,256]{2,1,0:T(8,128)(2,1)} %bitcast.12, bf16[2,64,256]{2,1,0:T(8,128)(2,1)} %bitcast.13, s32[16,512]{1,0:T(8,128)} %bitcast.14, ...), custom_call_target="tpu_custom_call" | custom-call | tf_op jit(solution)/shard_map/pallas_call | solution.py:659
  41.1 0.5 %slice.3 = f32[1,1]{1,0:T(1,128)} slice(f32[8,128]{1,0:T(8,128)S(1)} %get-tuple-element.5), slice={[0:1], [0:1]} | slice | bytes 8 | tf_op jit(solution)/shard_map/slice | solution.py:672
  41.6 0.7 %copy.14 = bf16[1,19,16,512]{3,2,1,0:T(8,128)(2,1)} copy(bf16[1,19,16,512]{3,2,1,0:T(8,128)(2,1)S(1)} %bitcast.9) | data formatting | bytes 622592

commit v4 on v3

--- a/solution.py
+++ b/solution.py
@@ -12,8 +12,8 @@
 IGNORED = 255
 Q_CHUNKS = 4
 E_CHUNKS = 2
-TICKS = (1, 1, 1, 1, 1, 1)
-PAIRS = (3, 2, 1, 2)
+TICKS = (2, 0, 0, 0, 0, 1, 0, 0, 0, 0, 2, 1, 0)
+PAIRS = (4, 4, 0)
 MESH = pl.DeviceIdType.MESH
 F32 = jnp.float32
 BF16 = jnp.bfloat16
@@ -46,33 +46,55 @@
     ).astype(BF16)
 
 
-def conv_block(lines, flat, rows):
+def from_left(taps, cols):
+    col = lax.rem(lax.broadcasted_iota(jnp.int32, taps.shape, 0), cols)
+    return jnp.where(col == 0, 0.0, pltpu.roll(taps, 1, 0))
+
+
+def from_right(taps, cols):
+    count = taps.shape[0]
+    col = lax.rem(lax.broadcasted_iota(jnp.int32, taps.shape, 0), cols)
+    return jnp.where(col == cols - 1, 0.0, pltpu.roll(taps, count - 1, 0))
+
+
+def keep(y, y_ref, stat_ref, row, offset):
+    y_ref[row + offset] = y
+    sums = jnp.sum(y, axis=0, keepdims=True)
+    centred = y - sums / y.shape[0]
+    stat_ref[row, 0:1] = sums
+    stat_ref[row, 1:2] = jnp.sum(centred * centred, axis=0, keepdims=True)
+
+
+def conv_to(x_ref, weights, y_ref, stat_ref, start, pairs, offset):
+    flat, both = weights
+    cols, depth = x_ref.shape[1:]
     width = flat.shape[1] // 3
-    count = lines.shape[0]
-    cols = count // rows
-    taps = jnp.dot(lines, flat, preferred_element_type=F32)
-    col = lax.rem(lax.broadcasted_iota(jnp.int32, (count, width), 0), cols)
-    left = jnp.where(col == 0, 0.0, pltpu.roll(taps[:, :width], 1, 0))
-    right = jnp.where(col == cols - 1, 0.0, pltpu.roll(taps[:, 2 * width :], count - 1, 0))
-    return (taps[:, width : 2 * width] + left + right).reshape(rows, cols, width)
-
-
-def keep(y, y_ref, stat_ref, start, offset):
-    rows, cols = y.shape[:2]
-    y_ref[pl.ds(start + offset, rows)] = y
-    sums = jnp.sum(y, axis=1, keepdims=True)
-    centred = y - sums / cols
-    stat_ref[pl.ds(start, rows), 0:1] = sums
-    stat_ref[pl.ds(start, rows), 1:2] = jnp.sum(centred * centred, axis=1, keepdims=True)
-
-
-def conv_to(x_ref, flat_ref, y_ref, stat_ref, start, rows, offset):
-    cols, depth = x_ref.shape[1:]
-    lines = [
-        x_ref[pl.ds(start + down, rows)].reshape(rows * cols, depth) for down in range(3)
-    ]
-    y = conv_block(jnp.concatenate(lines, axis=1), flat_ref[...], rows)
-    keep(y, y_ref, stat_ref, start, offset)
+    lines = jnp.concatenate(
+        [
+            jnp.concatenate([x_ref[start + 2 * k + down] for k in range(pairs)], axis=0)
+            for down in range(4)
+        ],
+        axis=1,
+    )
+    first = jnp.dot(lines[:, : 3 * depth], flat[:, : 2 * width], preferred_element_type=F32)
+    shared = jnp.dot(lines, both[...], preferred_element_type=F32)
+    last = jnp.dot(lines[:, depth:], flat[:, width:], preferred_element_type=F32)
+    upper = first[:, width:] + from_left(first[:, :width], cols) + from_right(shared[:, :width], cols)
+    lower = last[:, :width] + from_left(shared[:, width:], cols) + from_right(last[:, width:], cols)
+    for k in range(pairs):
+        for row, y in ((0, upper), (1, lower)):
+            keep(y[k * cols : (k + 1) * cols], y_ref, stat_ref, start + 2 * k + row, offset)
+
+
+def border_term(line, flat):
+    width = flat.shape[1] // 3
+    taps = jnp.dot(line, flat, preferred_element_type=F32)
+    cols = line.shape[0]
+    return (
+        taps[:, width : 2 * width]
+        + from_left(taps[:, :width], cols)
+        + from_right(taps[:, 2 * width :], cols)
+    )
 
 
 def head_kernel(
@@ -80,9 +102,10 @@
     q, e, s, t, labels_in, first_w, inner_w, gain_in, shift_in, class_w_in, bias_in,
     out, loss_out,
     labels, gain, shift, class_w, bias,
-    q_in, e_in, s_in, t_in, w_q, w_e, w_s, w_t, w_i,
+    q_in, e_in, s_in, t_in, w_q, w_e, w_s, w_t, w_i, b_q, b_e, b_s, b_t, b_i,
     q_y, e_y, s_y, t_y, s_grown, s_y2, t_grown, t_y2, t_grown2, t_y3,
-    t_leave, s_leave, t_leave2, e_leave, q_leave, t_land, s_land, t_land2, e_land, q_land,
+    t_leave, s_leave, t_leave2, t_leave3, t_lent, s_lent, e_lent, q_lent,
+    t_land, s_land, t_land2, t_land3, t_owed, s_owed, e_owed, q_owed,
     base_leave, base_land,
     q_stat, e_stat, s_stat, t_stat, s_stat2, t_stat2, t_stat3,
     slab, slabs, class_f, class_pad, up_t, up_s, coarse, wide, scores, loss_slab, loss_slabs,
@@ -95,20 +118,21 @@
     width = q_y.shape[2]
     classes = class_w.shape[0]
 
-    def device_at(distance):
-        number = lax.rem(flat + distance, total)
-        return {"batch": lax.div(number, size), "rows": lax.rem(number, size)}
+    def wrapped(place, distance, count):
+        place = place + distance
+        return jnp.where(place >= count, place - count, place)
+
+    peers = [
+        {"batch": wrapped(image, across, images), "rows": wrapped(me, along, size)}
+        for across in range(images)
+        for along in range(size)
+        if across or along
+    ]
 
     phase("enter")
     barrier = pltpu.get_barrier_semaphore()
-
-    def greet(distance, carry):
-        pl.semaphore_signal(
-            barrier, inc=1, device_id=device_at(distance), device_id_type=MESH
-        )
-        return carry
-
-    lax.fori_loop(1, total, greet, 0)
+    for peer in peers:
+        pl.semaphore_signal(barrier, inc=1, device_id=peer, device_id_type=MESH)
 
     fetched = []
 
@@ -118,17 +142,27 @@
         fetched.append(copy)
         return copy
 
-    def fetch_weights(source, target):
-        depth = source.shape[2]
+    def block(ref, down, column):
+        depth = ref.shape[0] // (3 if ref.shape[1] == 3 * width else 4)
+        return ref.at[down * depth : (down + 1) * depth, column * width : (column + 1) * width]
+
+    def fetch_flat(source, target):
         done = local_sem.at[len(fetched)]
         for down in range(3):
             for across in range(3):
-                place = target.at[
-                    down * depth : (down + 1) * depth, across * width : (across + 1) * width
-                ]
+                place = block(target, down, across)
                 pltpu.make_async_copy(source.at[down, across], place, done).start()
         fetched.append(pltpu.make_async_copy(target, target, done))
-        return [fetched[-1]]
+        return fetched[-1:]
+
+    def fetch_both(source, target):
+        done = local_sem.at[len(fetched)]
+        for down in range(3):
+            pltpu.make_async_copy(source.at[down, 2], block(target, down, 0), done).start()
+            pltpu.make_async_copy(source.at[down, 0], block(target, down + 1, 1), done).start()
+        part = target.at[0 : 3 * source.shape[2]]
+        fetched.append(pltpu.make_async_copy(part, part, done))
+        return fetched[-1:]
 
     def settle(copies):
         for copy in copies:
@@ -137,11 +171,13 @@
     q_rows, q_cols = q.shape[:2]
     e_rows, s_rows, t_rows = e.shape[0], s.shape[0], t.shape[0]
     e_cols, s_cols, t_cols = e.shape[1], s.shape[1], t.shape[1]
-    got_t = [fetch(t, t_in.at[1 : t_rows + 1])]
-    got_s = [fetch(s, s_in.at[1 : s_rows + 1])]
-    got_q = fetch_weights(first_w.at[0], w_q) + [fetch(q, q_in.at[1 : q_rows + 1])]
-    got_w_t = fetch_weights(first_w.at[3], w_t)
-    got_w_s = fetch_weights(first_w.at[2], w_s)
+    got_t = [fetch(t, t_in.at[1 : t_rows + 1])] + fetch_flat(first_w.at[3], w_t)
+    got_s = [fetch(s, s_in.at[1 : s_rows + 1])] + fetch_flat(first_w.at[2], w_s)
+    got_q = fetch_flat(first_w.at[0], w_q) + [fetch(q, q_in.at[1 : q_rows + 1])]
+    got_e = fetch_flat(first_w.at[1], w_e) + [fetch(e, e_in.at[1 : e_rows + 1])]
+    got_b_q = fetch_both(first_w.at[0], b_q)
+    got_b_t = fetch_both(first_w.at[3], b_t)
+    got_b_s = fetch_both(first_w.at[2], b_s)
     got_small = [
         fetch(class_w_in, class_w),
         fetch(bias_in, bias),
@@ -149,8 +185,10 @@
         fetch(shift_in, shift),
         fetch(labels_in, labels),
     ]
-    got_i = [fetch_weights(inner_w.at[i], w_i.at[i]) for i in range(3)]
-    got_e = fetch_weights(first_w.at[1], w_e) + [fetch(e, e_in.at[1 : e_rows + 1])]
+    got_i = [
+        fetch_flat(inner_w.at[i], w_i.at[i]) + fetch_both(inner_w.at[i], b_i.at[i]) for i in range(3)
+    ]
+    got_b_e = fetch_both(first_w.at[1], b_e)
 
     def exists(offset):
         return me + offset < size if offset > 0 else me + offset >= 0
@@ -193,9 +231,10 @@
     def line_edges(leaving, landing, number):
         return edges(leaving.at[1], leaving.at[0], landing.at[0], landing.at[1], number)
 
-    t_edges, s_edges = band_edges(t_in, 0), band_edges(s_in, 2)
+    t_edges, s_edges = line_edges(t_lent, t_owed, 0), line_edges(s_lent, s_owed, 2)
     t_y_edges, s_y_edges = line_edges(t_leave, t_land, 4), line_edges(s_leave, s_land, 6)
-    t_y2_edges, coarse_edges = line_edges(t_leave2, t_land2, 8), band_edges(coarse, 10)
+    t_y2_edges, t_y3_edges = line_edges(t_leave2, t_land2, 8), line_edges(t_leave3, t_land3, 20)
+    coarse_edges = band_edges(coarse, 10)
 
     def part_edges(leaving, landing, number, chunks):
         step = leaving.shape[1] // chunks
@@ -206,37 +245,55 @@
             for part in (pl.ds(k * step, step) for k in range(chunks))
         ]
 
-    e_edges, q_edges = line_edges(e_leave, e_land, 12), line_edges(q_leave, q_land, 14)
-    base_edges = line_edges(base_leave, base_land, 16)
-    chunks = part_edges(e_leave, e_land, 12, E_CHUNKS) + part_edges(q_leave, q_land, 14, Q_CHUNKS)
+    e_edges, q_edges = line_edges(e_lent, e_owed, 12), line_edges(q_lent, q_owed, 14)
+    coarse_base = line_edges(base_leave.at[0], base_land.at[0], 16)
+    fine_base = line_edges(base_leave.at[1], base_land.at[1], 18)
+    chunks = part_edges(e_lent, e_owed, 12, E_CHUNKS) + part_edges(q_lent, q_owed, 14, Q_CHUNKS)
     waiting, ticks = list(chunks), list(TICKS)
 
     def tick():
         for _ in range(ticks.pop(0)):
             send(waiting.pop(0))
 
-    @pl.when(me == 0)
-    def _():
-        for field in (s_in, t_in):
-            field[0] = jnp.zeros(field.shape[1:], BF16)
-
-    @pl.when(me == size - 1)
-    def _():
-        for field in (s_in, t_in):
-            field[field.shape[0] - 1] = jnp.zeros(field.shape[1:], BF16)
-
-    for field in (q_in, e_in):
+    for both in (b_q, b_e, b_s, b_t, *[b_i.at[i] for i in range(3)]):
+        depth = both.shape[0] // 4
+        for row, column in ((3 * depth, 0), (0, width)):
+            both[row : row + depth, column : column + width] = jnp.zeros((depth, width), BF16)
+
+    for field in (q_in, e_in, s_in, t_in):
         for row in (0, field.shape[0] - 1):
             field[row] = jnp.zeros(field.shape[1:], BF16)
 
     up_t[...] = doubling(*up_t.shape, 1)
     up_s[...] = doubling(*up_s.shape, 1)
 
+    def lend(x_ref, flat_ref, lent, kind, place):
+        depth, last = x_ref.shape[2], x_ref.shape[0] - 2
+        for side, row, down in ((0, 1, 2), (1, last, 0)):
+            term = border_term(x_ref[row], flat_ref[down * depth : (down + 1) * depth])
+            base = jnp.sum(term, axis=0, keepdims=True) / term.shape[0]
+            lent[side] = (term - base).astype(BF16)
+            base_leave[kind, side, place : place + 1] = base
+
+    phase("lend_t")
+    settle(got_t)
+    lend(t_in, w_t, t_lent, 0, 0)
+    phase("lend_s")
+    settle(got_s)
+    lend(s_in, w_s, s_lent, 0, 1)
+    phase("lend_q")
+    settle(got_q)
+    lend(q_in, w_q, q_lent, 1, 0)
     phase("barrier")
     pl.semaphore_wait(barrier, total - 1)
-    phase("send_ts")
-    settle(got_t)
     send(t_edges)
+    send(coarse_base)
+    send(s_edges)
+    phase("lend_e")
+    settle(got_e)
+    lend(e_in, w_e, e_lent, 1, 1)
+    send(fine_base)
+    tick()
 
     def slab_copy(number, distance, sender):
         return pltpu.make_async_remote_copy(
@@ -332,15 +389,13 @@
         def _():
             grown[2 * own + 1] = jnp.zeros(grown.shape[1:], BF16)
 
-    def convolve(x_ref, flat_ref, y_ref, stat_ref, offset):
+    def convolve(x_ref, weights, y_ref, stat_ref, offset):
         count, cols = x_ref.shape[0] - 2, x_ref.shape[1]
-        rows = max(r for r in range(1, count + 1) if count % r == 0 and (r == 1 or r * cols <= 1024))
-
-        def step(index, carry):
-            conv_to(x_ref, flat_ref, y_ref, stat_ref, index * rows, rows, offset)
-            return carry
-
-        lax.fori_loop(0, count // rows, step, 0)
+        pairs = max(
+            r for r in range(1, count // 2 + 1) if count % (2 * r) == 0 and (r == 1 or r * cols <= 512)
+        )
+        for index in range(count // (2 * pairs)):
+            conv_to(x_ref, weights, y_ref, stat_ref, 2 * pairs * index, pairs, offset)
 
     done, pairs_left = [0], list(PAIRS)
 
@@ -348,62 +403,42 @@
         first, last = done[0], done[0] + pairs_left.pop(0)
         done[0] = last = last if pairs_left else q_rows // 2
 
-        def step(index, carry):
-            conv_to(q_in, w_q, q_y, q_stat, 2 * index, 2, 0)
-            return carry
-
-        lax.fori_loop(first, last, step, 0)
-
-    def lend(x_ref, flat_ref, leaving, place):
-        depth, last = x_ref.shape[2], x_ref.shape[0] - 2
-        for side, row, down in ((0, 1, 2), (1, last, 0)):
-            flat = flat_ref[down * depth : (down + 1) * depth]
-            term = conv_block(x_ref[row], flat, 1)[0]
-            base = jnp.sum(term, axis=0, keepdims=True) / term.shape[0]
-            leaving[side] = (term - base).astype(BF16)
-            base_leave[side, place : place + 1] = base
-
-    def mend(y_ref, stat_ref, landing, place, pairs):
+        for index in range(first, last):
+            conv_to(q_in, (w_q, b_q), q_y, q_stat, 2 * index, 1, 0)
+            tick()
+
+    def mend(y_ref, stat_ref, owed, kind, place, pairs, offset):
         arrive(pairs)
 
         def add(side, row):
-            term = landing[side].astype(F32) + base_land[side, place : place + 1]
-            keep((y_ref[row] + term)[None], y_ref, stat_ref, row, 0)
+            term = owed[side].astype(F32) + base_land[kind, side, place : place + 1]
+            keep(y_ref[row + offset] + term, y_ref, stat_ref, row, offset)
 
         pl.when(me > 0)(lambda: add(0, 0))
-        pl.when(me < size - 1)(lambda: add(1, y_ref.shape[0] - 1))
-
-    phase("fetch_q")
-    settle(got_q)
-    phase("lend_q")
-    lend(q_in, w_q, q_leave, 0)
-    settle(got_s)
-    send(s_edges)
+        pl.when(me < size - 1)(lambda: add(1, stat_ref.shape[0] - 1))
+
     phase("q_blocks_a")
+    settle(got_b_q)
     q_blocks()
-    phase("lend_e")
-    settle(got_e)
-    lend(e_in, w_e, e_leave, 1)
-    send(base_edges)
-    tick()
-    phase("wait_t")
-    settle(got_w_t)
-    arrive(t_edges)
     phase("conv_t")
-    conv_to(t_in, w_t, t_y, t_stat, 0, t_rows, 1)
+    settle(got_b_t)
+    convolve(t_in, (w_t, b_t), t_y, t_stat, 1)
+    phase("mend_t")
+    arrive(coarse_base)
+    mend(t_y, t_stat, t_owed, 0, 0, t_edges, 1)
     phase("announce_t")
     announce(0, t_stat, t_cols)
     part_with(t_y, t_leave, 0, t_y_edges)
-    phase("wait_s")
-    settle(got_w_s)
-    arrive(s_edges)
     phase("conv_s")
-    conv_to(s_in, w_s, s_y, s_stat, 0, s_rows, 1)
+    settle(got_b_s)
+    convolve(s_in, (w_s, b_s), s_y, s_stat, 1)
+    phase("mend_s")
+    mend(s_y, s_stat, s_owed, 0, 1, s_edges, 1)
     announce(1, s_stat, s_cols)
     part_with(s_y, s_leave, 1, s_y_edges)
+    settle(got_small)
     tick()
     phase("q_blocks_b")
-    settle(got_small)
     q_blocks()
     phase("gather_t")
     norm = gather(0, t_rows, t_cols)
@@ -413,11 +448,21 @@
     phase("grow_t")
     grow(t_y, t_grown, up_t, activation(norm, 3))
     phase("conv_t2")
-    convolve(t_grown, w_i.at[1], t_y2, t_stat2, 1)
+    convolve(t_grown, (w_i.at[1], b_i.at[1]), t_y2, t_stat2, 1)
     phase("announce_t2")
     announce(2, t_stat2, 2 * t_cols)
     part_with(t_y2, t_leave2, 2, t_y2_edges)
     tick()
+    phase("conv_e")
+    settle(got_b_e)
+    convolve(e_in, (w_e, b_e), e_y, e_stat, 0)
+    phase("mend_e")
+    arrive(fine_base)
+    mend(e_y, e_stat, e_owed, 1, 1, e_edges, 0)
+    announce(5, e_stat, e_cols)
+    tick()
+    phase("q_blocks_c")
+    q_blocks()
     phase("gather_s")
     norm = gather(1, s_rows, s_cols)
     settle(got_i[0])
@@ -426,38 +471,24 @@
     phase("grow_s")
     grow(s_y, s_grown, up_s, activation(norm, 2))
     phase("conv_s2")
-    convolve(s_grown, w_i.at[0], s_y2, s_stat2, 0)
+    convolve(s_grown, (w_i.at[0], b_i.at[0]), s_y2, s_stat2, 0)
     announce(3, s_stat2, 2 * s_cols)
     tick()
-    phase("q_blocks_c")
-    q_blocks()
     phase("gather_t2")
     norm = gather(2, 2 * t_rows, 2 * t_cols)
     settle(got_i[2])
-    tick()
     phase("frame_t2")
     frame(t_y2, t_land2, 2, t_y2_edges)
     phase("grow_t2")
     grow(t_y2, t_grown2, up_s, activation(norm, 5))
     phase("conv_t3")
-    convolve(t_grown2, w_i.at[2], t_y3, t_stat3, 0)
+    convolve(t_grown2, (w_i.at[2], b_i.at[2]), t_y3, t_stat3, 1)
     phase("announce_t3")
     announce(4, t_stat3, 4 * t_cols)
-    tick()
-    phase("wait_e")
-    convolve(e_in, w_e, e_y, e_stat, 0)
-    arrive(base_edges)
-    phase("mend_e")
-    mend(e_y, e_stat, e_land, 1, e_edges)
-    announce(5, e_stat, e_cols)
-    phase("q_blocks_d")
-    q_blocks()
+    part_with(t_y3, t_leave3, 4, t_y3_edges)
     phase("mend_q")
-    mend(q_y, q_stat, q_land, 0, q_edges)
+    mend(q_y, q_stat, q_owed, 1, 0, q_edges, 0)
     announce(6, q_stat, q_cols)
-
-    phase("gather_t3")
-    t_act = activation(gather(4, 4 * t_rows, 4 * t_cols), 6)
     phase("gather_se")
     s_act = activation(gather(3, 2 * s_rows, 2 * s_cols), 4)
     e_act = activation(gather(5, e_rows, e_cols), 1)
@@ -467,15 +498,15 @@
     class_pad[...] = class_f[...].astype(BF16)
     padded = class_f.shape[0]
     weight = class_pad[...]
-    weights = jnp.concatenate([weight] * 3, axis=1)
+    weights = jnp.concatenate([weight] * 2, axis=1)
     across = (((1,), (1,)), ((), ()))
 
     def project(row, carry):
-        lines = jnp.concatenate([e_act(e_y[row]), s_act(s_y2[row]), t_act(t_y3[row])], axis=1)
+        lines = jnp.concatenate([e_act(e_y[row]), s_act(s_y2[row])], axis=1)
         coarse[row + 1] = lax.dot_general(weights, lines, across, preferred_element_type=F32)
         return carry
 
-    lax.fori_loop(0, e_rows, project, 0, unroll=2)
+    lax.fori_loop(0, e_rows, project, 0, unroll=4)
     send(coarse_edges)
 
     phase("gather_q")
@@ -495,6 +526,7 @@
     phase("wait_coarse")
     up_cols = doubling(e_cols, q_cols, 0)
     arrive(coarse_edges)
+    leave(coarse_edges)
 
     @pl.when(me == 0)
     def _():
@@ -504,6 +536,19 @@
     def _():
         coarse[e_rows + 1] = coarse[e_rows]
 
+    phase("gather_t3")
+    t_act = activation(gather(4, 4 * t_rows, 4 * t_cols), 6)
+    phase("frame_t3")
+    frame(t_y3, t_land3, 4, t_y3_edges)
+    phase("project_t")
+
+    def project_t(row, carry):
+        coarse[row] += lax.dot_general(
+            weight, t_act(t_y3[row]), across, preferred_element_type=F32
+        )
+        return carry
+
+    lax.fori_loop(0, e_rows + 2, project_t, 0, unroll=True)
     phase("widen")
     lines = coarse[...].reshape((e_rows + 2) * padded, e_cols)
     high = lines.astype(BF16)
@@ -539,24 +584,20 @@
             line[:, k * width : (k + 1) * width] for k in range(q_cols // width)
         )
 
-    def loss_copy(source, target, distance):
+    def loss_copy(source, target, peer):
         return pltpu.make_async_remote_copy(
             src_ref=source,
             dst_ref=target,
             send_sem=loss_send.at[0],
             recv_sem=loss_recv.at[0],
-            device_id=device_at(distance),
+            device_id=peer,
             device_id_type=MESH,
         )
 
-    def loss_go(distance, carry):
-        loss_copy(loss_slab, loss_slabs.at[flat], distance).start()
-        return carry
-
+    for peer in reversed(peers):
+        loss_copy(loss_slab, loss_slabs.at[flat], peer).start()
     rest = loss_slabs.at[0 : total - 1]
-    loss_all = loss_copy(rest, rest, 1)
-
-    lax.fori_loop(1, total, loss_go, 0)
+    loss_all = loss_copy(rest, rest, peers[0])
     loss_slabs[flat] = loss_slab[...]
     phase("output")
     for first in range(0, classes, 8):
@@ -564,7 +605,7 @@
         out[first : min(first + 8, classes)] = lines[: min(8, classes - first)]
     phase("leave")
     for pairs in (
-        t_edges, s_edges, t_y_edges, s_y_edges, t_y2_edges, coarse_edges, e_edges, q_edges, base_edges,
+        t_edges, s_edges, t_y_edges, s_y_edges, t_y2_edges, t_y3_edges, e_edges, q_edges, coarse_base, fine_base,
     ):
         leave(pairs)
     for number in range(slab.shape[0]):
@@ -622,6 +663,8 @@
             framed(t_rows, t_cols, depth),
             *[pltpu.VMEM((3 * depth, 3 * width), BF16)] * 4,
             pltpu.VMEM((3, 3 * width, 3 * width), BF16),
+            *[pltpu.VMEM((4 * depth, 2 * width), BF16)] * 4,
+            pltpu.VMEM((3, 4 * width, 2 * width), BF16),
             field(q_rows, q_cols),
             field(e_rows, e_cols),
             framed(s_rows, s_cols, width, F32),
@@ -631,9 +674,13 @@
             framed(2 * t_rows, 2 * t_cols, width),
             framed(2 * t_rows, 2 * t_cols, width, F32),
             framed(4 * t_rows, 4 * t_cols, width),
-            field(4 * t_rows, 4 * t_cols),
-            *[line(cols) for cols in (t_cols, s_cols, 2 * t_cols, e_cols, q_cols)] * 2,
-            *[pltpu.VMEM((2, 2, width), F32)] * 2,
+            framed(4 * t_rows, 4 * t_cols, width, F32),
+            *[
+                line(c)
+                for c in (t_cols, s_cols, 2 * t_cols, 4 * t_cols, t_cols, s_cols, e_cols, q_cols)
+            ]
+            * 2,
+            *[pltpu.VMEM((2, 2, 2, width), F32)] * 2,
             stat(q_rows),
             stat(e_rows),
             stat(s_rows),
@@ -652,7 +699,7 @@
             pltpu.VMEM((q_rows, padded, q_cols), F32),
             pltpu.VMEM((2, width), F32),
             pltpu.VMEM((total, 2, width), F32),
-            *[pltpu.SemaphoreType.DMA((count,)) for count in (17, 18, 18, 7, 7, 1, 1)],
+            *[pltpu.SemaphoreType.DMA((count,)) for count in (32, 22, 22, 7, 7, 1, 1)],
         ]
         away, held = pl.BlockSpec(memory_space=pl.ANY), pl.BlockSpec(memory_space=pltpu.VMEM)
         operands = (q, e, s, t, small[0], first_weights, inner_weights, *small[1:])

time: 42.5 us -> 39.2 us (0.922)
  Pallas kernels: 40.5 us -> 37.2 us
    pallas_call x1, Pallas kernels: 40.5 us -> 37.2 us  [per_device(): pl.pallas_call(functools.partial(head_kernel, shape), out_shape=(jax.Shap...]
where the time goes in v4:
time: 39.2 us; the launch traced here: 39 us
  Pallas kernels  37.2 us (95%)
  local copies, waits for them, and re-layouts  1.23 us (3%)
  between operations  0.64 us (2%)
    pallas_call x1, Pallas kernels, per_device(): pl.pallas_call(functools.partial(head_kernel, shape), out_shape=(jax.Shap...  37.2 us

profile of v4, /device:TPU:0, one launch (start us, length us, event | category | flops | bytes accessed | tf_op | source)
XLA Modules:
  0.0 39.0 jit_solution(15511702729001326511)
XLA Ops:
  0.6 37.2 %shard_map.122 = (bf16[19,16,512]{2,1,0:T(8,128)(2,1)S(1)}, f32[8,128]{1,0:T(8,128)S(1)}) custom-call(bf16[16,512,256]{2,1,0:T(8,128)(2,1)} %bitcast.10, bf16[8,256,256]{2,1,0:T(8,128)(2,1)} %bitcast.11, bf16[4,128,256]{2,1,0:T(8,128)(2,1)} %bitcast.12, bf16[2,64,256]{2,1,0:T(8,128)(2,1)} %bitcast.13, s32[16,512]{1,0:T(8,128)} %bitcast.14, ...), custom_call_target="tpu_custom_call" | custom-call | tf_op jit(solution)/shard_map/pallas_call | solution.py:706
  37.8 0.5 %slice.3 = f32[1,1]{1,0:T(1,128)} slice(f32[8,128]{1,0:T(8,128)S(1)} %get-tuple-element.5), slice={[0:1], [0:1]} | slice | bytes 8 | tf_op jit(solution)/shard_map/slice | solution.py:719
  38.3 0.7 %copy.14 = bf16[1,19,16,512]{3,2,1,0:T(8,128)(2,1)} copy(bf16[1,19,16,512]{3,2,1,0:T(8,128)(2,1)S(1)} %bitcast.9) | data formatting | bytes 622592

commit v5 on v4

--- a/solution.py
+++ b/solution.py
@@ -12,8 +12,8 @@
 IGNORED = 255
 Q_CHUNKS = 4
 E_CHUNKS = 2
-TICKS = (2, 0, 0, 0, 0, 1, 0, 0, 0, 0, 2, 1, 0)
-PAIRS = (4, 4, 0)
+TICKS = (2, 0, 0, 0, 0, 1, 1, 0, 0, 2, 0, 0, 0)
+PAIRS = (4, 1, 3)
 MESH = pl.DeviceIdType.MESH
 F32 = jnp.float32
 BF16 = jnp.bfloat16
@@ -106,7 +106,7 @@
     q_y, e_y, s_y, t_y, s_grown, s_y2, t_grown, t_y2, t_grown2, t_y3,
     t_leave, s_leave, t_leave2, t_leave3, t_lent, s_lent, e_lent, q_lent,
     t_land, s_land, t_land2, t_land3, t_owed, s_owed, e_owed, q_owed,
-    base_leave, base_land,
+    base_leave, base_land, rim_leave, rim_land,
     q_stat, e_stat, s_stat, t_stat, s_stat2, t_stat2, t_stat3,
     slab, slabs, class_f, class_pad, up_t, up_s, coarse, wide, scores, loss_slab, loss_slabs,
     local_sem, edge_send, edge_recv, slab_send, slab_recv, loss_send, loss_recv,
@@ -234,7 +234,7 @@
     t_edges, s_edges = line_edges(t_lent, t_owed, 0), line_edges(s_lent, s_owed, 2)
     t_y_edges, s_y_edges = line_edges(t_leave, t_land, 4), line_edges(s_leave, s_land, 6)
     t_y2_edges, t_y3_edges = line_edges(t_leave2, t_land2, 8), line_edges(t_leave3, t_land3, 20)
-    coarse_edges = band_edges(coarse, 10)
+    coarse_edges = line_edges(rim_leave, rim_land, 10)
 
     def part_edges(leaving, landing, number, chunks):
         step = leaving.shape[1] // chunks
@@ -438,6 +438,14 @@
     part_with(s_y, s_leave, 1, s_y_edges)
     settle(got_small)
     tick()
+    phase("conv_e")
+    settle(got_b_e)
+    convolve(e_in, (w_e, b_e), e_y, e_stat, 0)
+    phase("mend_e")
+    arrive(fine_base)
+    mend(e_y, e_stat, e_owed, 1, 1, e_edges, 0)
+    announce(5, e_stat, e_cols)
+    tick()
     phase("q_blocks_b")
     q_blocks()
     phase("gather_t")
@@ -453,16 +461,6 @@
     announce(2, t_stat2, 2 * t_cols)
     part_with(t_y2, t_leave2, 2, t_y2_edges)
     tick()
-    phase("conv_e")
-    settle(got_b_e)
-    convolve(e_in, (w_e, b_e), e_y, e_stat, 0)
-    phase("mend_e")
-    arrive(fine_base)
-    mend(e_y, e_stat, e_owed, 1, 1, e_edges, 0)
-    announce(5, e_stat, e_cols)
-    tick()
-    phase("q_blocks_c")
-    q_blocks()
     phase("gather_s")
     norm = gather(1, s_rows, s_cols)
     settle(got_i[0])
@@ -474,6 +472,8 @@
     convolve(s_grown, (w_i.at[0], b_i.at[0]), s_y2, s_stat2, 0)
     announce(3, s_stat2, 2 * s_cols)
     tick()
+    phase("q_blocks_c")
+    q_blocks()
     phase("gather_t2")
     norm = gather(2, 2 * t_rows, 2 * t_cols)
     settle(got_i[2])
@@ -507,34 +507,12 @@
         return carry
 
     lax.fori_loop(0, e_rows, project, 0, unroll=4)
+    rim_leave[0] = coarse[1].astype(BF16)
+    rim_leave[1] = coarse[e_rows].astype(BF16)
     send(coarse_edges)
-
-    phase("gather_q")
-    q_act = activation(gather(6, q_rows, q_cols), 0)
-    spot = lax.broadcasted_iota(jnp.int32, (padded, classes), 0)
-    lane = lax.broadcasted_iota(jnp.int32, (padded, classes), 1)
-    bias_col = jnp.sum(jnp.where(spot == lane, bias[...], 0.0), axis=1, keepdims=True)
-    phase("score_q")
-
-    def score(row, carry):
-        scores[row] = (
-            lax.dot_general(weight, q_act(q_y[row]), across, preferred_element_type=F32) + bias_col
-        )
-        return carry
-
-    lax.fori_loop(0, q_rows, score, 0, unroll=4)
-    phase("wait_coarse")
+    coarse[0] = jnp.zeros(coarse.shape[1:], F32)
+    coarse[e_rows + 1] = jnp.zeros(coarse.shape[1:], F32)
     up_cols = doubling(e_cols, q_cols, 0)
-    arrive(coarse_edges)
-    leave(coarse_edges)
-
-    @pl.when(me == 0)
-    def _():
-        coarse[0] = coarse[1]
-
-    @pl.when(me == size - 1)
-    def _():
-        coarse[e_rows + 1] = coarse[e_rows]
 
     phase("gather_t3")
     t_act = activation(gather(4, 4 * t_rows, 4 * t_cols), 6)
@@ -549,6 +527,18 @@
         return carry
 
     lax.fori_loop(0, e_rows + 2, project_t, 0, unroll=True)
+    phase("wait_coarse")
+    arrive(coarse_edges)
+    for beyond, row, own, side in ((me == 0, 0, 1, 0), (me == size - 1, e_rows + 1, e_rows, 1)):
+
+        @pl.when(beyond)
+        def _():
+            coarse[row] = coarse[own]
+
+        @pl.when(jnp.logical_not(beyond))
+        def _():
+            coarse[row] += rim_land[side].astype(F32)
+
     phase("widen")
     lines = coarse[...].reshape((e_rows + 2) * padded, e_cols)
     high = lines.astype(BF16)
@@ -557,11 +547,17 @@
         low, up_cols, preferred_element_type=F32
     )
     wide[...] = lines.reshape(wide.shape)
+    phase("gather_q")
+    spot = lax.broadcasted_iota(jnp.int32, (padded, classes), 0)
+    lane = lax.broadcasted_iota(jnp.int32, (padded, classes), 1)
+    bias_col = jnp.sum(jnp.where(spot == lane, bias[...], 0.0), axis=1, keepdims=True)
+    q_act = activation(gather(6, q_rows, q_cols), 0)
     phase("finish")
     kind = lax.broadcasted_iota(jnp.int32, (padded, q_cols), 0)
 
     def finish(row, grown):
-        line = scores[row] + grown
+        line = lax.dot_general(weight, q_act(q_y[row]), across, preferred_element_type=F32)
+        line = line + bias_col + grown
         scores[row] = line
         powers = jnp.where(kind < classes, jnp.exp(line), 0.0)
         log_total = jnp.log(jnp.sum(powers, axis=0, keepdims=True))
@@ -577,7 +573,7 @@
         return carry[0] + upper[0] + lower[0], carry[1] + upper[1] + lower[1]
 
     zero = jnp.zeros((1, q_cols), F32)
-    sums = lax.fori_loop(0, e_rows, pair, (zero, zero), unroll=2)
+    sums = lax.fori_loop(0, e_rows, pair, (zero, zero), unroll=4)
     phase("loss_send")
     for place, line in enumerate(sums):
         loss_slab[place : place + 1] = sum(
@@ -605,7 +601,7 @@
         out[first : min(first + 8, classes)] = lines[: min(8, classes - first)]
     phase("leave")
     for pairs in (
-        t_edges, s_edges, t_y_edges, s_y_edges, t_y2_edges, t_y3_edges, e_edges, q_edges, coarse_base, fine_base,
+        t_edges, s_edges, t_y_edges, s_y_edges, t_y2_edges, t_y3_edges, coarse_edges, e_edges, q_edges, coarse_base, fine_base,
     ):
         leave(pairs)
     for number in range(slab.shape[0]):
@@ -681,6 +677,7 @@
             ]
             * 2,
             *[pltpu.VMEM((2, 2, 2, width), F32)] * 2,
+            *[pltpu.VMEM((2, padded, e_cols), BF16)] * 2,
             stat(q_rows),
             stat(e_rows),
             stat(s_rows),

time: 39.2 us -> 38 us (0.969)
  Pallas kernels: 37.2 us -> 36 us
    pallas_call x1, Pallas kernels: 37.2 us -> 36 us  [per_device(): pl.pallas_call(functools.partial(head_kernel, shape), out_shape=(jax.Shap...]
where the time goes in v5:
time: 38 us; the launch traced here: 37.9 us
  Pallas kernels  36 us (95%)
  local copies, waits for them, and re-layouts  1.23 us (3%)
  between operations  0.64 us (2%)
    pallas_call x1, Pallas kernels, per_device(): pl.pallas_call(functools.partial(head_kernel, shape), out_shape=(jax.Shap...  36 us

profile of v5, /device:TPU:0, one launch (start us, length us, event | category | flops | bytes accessed | tf_op | source)
XLA Modules:
  0.0 37.9 jit_solution(16176433771759787148)
XLA Ops:
  0.6 36.0 %shard_map.122 = (bf16[19,16,512]{2,1,0:T(8,128)(2,1)S(1)}, f32[8,128]{1,0:T(8,128)S(1)}) custom-call(bf16[16,512,256]{2,1,0:T(8,128)(2,1)} %bitcast.10, bf16[8,256,256]{2,1,0:T(8,128)(2,1)} %bitcast.11, bf16[4,128,256]{2,1,0:T(8,128)(2,1)} %bitcast.12, bf16[2,64,256]{2,1,0:T(8,128)(2,1)} %bitcast.13, s32[16,512]{1,0:T(8,128)} %bitcast.14, ...), custom_call_target="tpu_custom_call" | custom-call | tf_op jit(solution)/shard_map/pallas_call | solution.py:703
  36.6 0.5 %slice.3 = f32[1,1]{1,0:T(1,128)} slice(f32[8,128]{1,0:T(8,128)S(1)} %get-tuple-element.5), slice={[0:1], [0:1]} | slice | bytes 8 | tf_op jit(solution)/shard_map/slice | solution.py:716
  37.1 0.7 %copy.14 = bf16[1,19,16,512]{3,2,1,0:T(8,128)(2,1)} copy(bf16[1,19,16,512]{3,2,1,0:T(8,128)(2,1)S(1)} %bitcast.9) | data formatting | bytes 622592

commit v6 on v5

--- a/solution.py
+++ b/solution.py
@@ -281,14 +281,14 @@
     phase("lend_s")
     settle(got_s)
     lend(s_in, w_s, s_lent, 0, 1)
-    phase("lend_q")
-    settle(got_q)
-    lend(q_in, w_q, q_lent, 1, 0)
     phase("barrier")
     pl.semaphore_wait(barrier, total - 1)
     send(t_edges)
     send(coarse_base)
     send(s_edges)
+    phase("lend_q")
+    settle(got_q)
+    lend(q_in, w_q, q_lent, 1, 0)
     phase("lend_e")
     settle(got_e)
     lend(e_in, w_e, e_lent, 1, 1)

time: 38 us -> 37.7 us (level)
  no operation moved by 1% of the time
where the time goes in v6:
time: 37.7 us; the launch traced here: 37.6 us
  Pallas kernels  35.7 us (95%)
  local copies, waits for them, and re-layouts  1.23 us (3%)
  between operations  0.64 us (2%)
    pallas_call x1, Pallas kernels, per_device(): pl.pallas_call(functools.partial(head_kernel, shape), out_shape=(jax.Shap...  35.7 us

profile of v6, /device:TPU:0, one launch (start us, length us, event | category | flops | bytes accessed | tf_op | source)
XLA Modules:
  0.0 37.6 jit_solution(10555485300606143425)
XLA Ops:
  0.6 35.7 %shard_map.122 = (bf16[19,16,512]{2,1,0:T(8,128)(2,1)S(1)}, f32[8,128]{1,0:T(8,128)S(1)}) custom-call(bf16[16,512,256]{2,1,0:T(8,128)(2,1)} %bitcast.10, bf16[8,256,256]{2,1,0:T(8,128)(2,1)} %bitcast.11, bf16[4,128,256]{2,1,0:T(8,128)(2,1)} %bitcast.12, bf16[2,64,256]{2,1,0:T(8,128)(2,1)} %bitcast.13, s32[16,512]{1,0:T(8,128)} %bitcast.14, ...), custom_call_target="tpu_custom_call" | custom-call | tf_op jit(solution)/shard_map/pallas_call | solution.py:703
  36.3 0.5 %slice.3 = f32[1,1]{1,0:T(1,128)} slice(f32[8,128]{1,0:T(8,128)S(1)} %get-tuple-element.5), slice={[0:1], [0:1]} | slice | bytes 8 | tf_op jit(solution)/shard_map/slice | solution.py:716
  36.8 0.7 %copy.14 = bf16[1,19,16,512]{3,2,1,0:T(8,128)(2,1)} copy(bf16[1,19,16,512]{3,2,1,0:T(8,128)(2,1)S(1)} %bitcast.9) | data formatting | bytes 622592
